TPU v7x, 512 devices: a whole 4x4x16 slice. The times are simulated.
512 devices in a mesh: rows: 128 (over z, y, core), cols: 4 (over x).
Axes of the slice: x: 4, y: 4, z: 16, core: 2. Of those that a mesh axis runs over, the one named last changes fastest.
Arguments:
- blocks: bfloat16 [512, 4, 3, 128, 128], P('rows', 'cols'), may hold values from -1.1953125 to 1.1953125
- block_cols: int32 [512, 4, 3], P('rows', 'cols'), may hold values from 0 to 511, as said below
Outputs:
- square_blocks: bfloat16 [512, 4, 36, 128, 128], P('rows', 'cols')
- square_cols: int32 [512, 4, 36], P('rows', 'cols')
- square_start: int32 [512, 4], P('rows', 'cols')
Inputs may be any that keep to these rules, and one draw needn't show every extreme that they name: Block-row i lies in panel p = i // 4; every block_cols[i, g, s] is a block-column congruent to g modulo 4 among block-rows 4 * (p - 4) to 4 * (p + 4) - 1, taken modulo 512; the three entries of one group differ; the block-columns i - 1, i and i + 1 (modulo 512) are always among a row's entries.
All inputs are finite; a program needn't handle non-finite values.
Results may differ from a plain program's by a relative error of at most 0.001.
Values may be sent and summed in bfloat16 or wider, within the bound.
No kernel may reach another device: no remote copies, remote signals or barrier semaphores. Data moves between devices by JAX's collectives and lax.ppermute only.
A program may use at most 64 MiB of HBM per device.

v0:
```python
import jax
import jax.numpy as jnp
from jax import lax
from jax.experimental import pallas as pl
from jax.experimental.pallas import tpu as pltpu
from jax.sharding import Mesh
from jax.sharding import PartitionSpec as P

HP = 4
PB = 4
KG = 3
GROUPS = 4
BS = 128
NP = 128
WIDTH = 36
USED = 15
WIN = 2 * HP
ROWS = ("rows_0", "rows_1", "rows_2")
ROOM = 16
FAR = 32
NEAR = 16
FAR_AXES = ("rows_0", "rows_2")
NEAR_AXES = ("rows_1", "cols")


def place():
    return lax.axis_index(ROWS), lax.axis_index("cols")


def spread_kernel(cols_ref, out_ref):
    lane = lax.broadcasted_iota(jnp.int32, (1, BS), 1)
    row = jnp.zeros((1, BS), jnp.int32)
    for r in range(PB):
        for s in range(KG):
            row = jnp.where(lane == KG * r + s, cols_ref[s, 0, r] >> 2, row)
    out_ref[...] = jnp.broadcast_to(row[None], out_ref.shape)


def turn_kernel(in_ref, out_ref, table_ref):
    p0, _ = place()
    table_ref[...] = jnp.zeros((NP, BS), jnp.int32)
    for n in range(FAR):
        spot = 8 * (n // 2) + (p0 & 6) + n % 2
        table_ref[pl.ds(spot, 1), :] = in_ref[n]
    turned = jnp.transpose(table_ref[...])
    out_ref[...] = jnp.broadcast_to(turned[None, :ROOM], out_ref.shape)


def bits_set(x):
    x = x - ((x >> 1) & 0x5555)
    x = (x & 0x3333) + ((x >> 2) & 0x3333)
    x = (x + (x >> 4)) & 0x0F0F
    return (x + (x >> 8)) & 0x1F


def index_kernel(tab_ref, cols_ref, starts_ref, map_ref, turned_ref):
    p0, c = place()
    spot = lax.broadcasted_iota(jnp.int32, (GROUPS * ROOM, NP), 1)
    parts = [tab_ref[GROUPS * n : GROUPS * (n + 1)] for n in range(NEAR // GROUPS)]
    turned = ((parts[0] + parts[1]) + (parts[2] + parts[3])).reshape(GROUPS * ROOM, NP)
    turned = (turned - spot + HP) & (NP - 1)
    turned_ref[...] = turned
    panel = lax.broadcasted_iota(jnp.int32, (1, NP), 1)
    wants = []
    owns = []
    for r in range(PB):
        want = jnp.zeros((1, NP), jnp.int32)
        for g in range(GROUPS):
            for s in range(KG):
                at = ROOM * g + KG * r + s
                want = want | jnp.left_shift(1, PB * turned_ref[at : at + 1, :] + g)
        wants.append(want)
        own = jnp.zeros((1, NP), jnp.int32)
        for s in range(KG):
            own = own | jnp.left_shift(1, turned_ref[pl.ds(ROOM * c + KG * r + s, 1), :])
        owns.append(own)
    pad = [jnp.zeros((PB, NP), jnp.int32)]
    want = jnp.concatenate(wants + pad, axis=0)
    own = jnp.concatenate(owns + pad, axis=0)
    found = jnp.zeros((8, NP), jnp.int32)
    for w in range(WIN):
        there = pltpu.roll(own, (HP - w) % NP, 1) if w != HP else own
        there = there << w
        for kr in range(PB):
            used = -((want >> (PB * w + kr)) & 1)
            found = found | (used & there[kr : kr + 1, :])
    counts = bits_set(found)
    before = jnp.sum(jnp.where(panel < p0, counts, 0).astype(jnp.float32)).astype(jnp.int32)
    here = jnp.where(panel == p0, 1, 0)
    mask = jnp.sum((found * here).astype(jnp.float32), axis=1, keepdims=True)
    count = jnp.sum((counts * here).astype(jnp.float32), axis=1, keepdims=True).astype(jnp.int32)
    mask = mask.astype(jnp.int32)
    lane = lax.broadcasted_iota(jnp.int32, (8, BS), 1)
    held = jnp.where(lane < 16, (jnp.broadcast_to(mask, (8, BS)) >> (lane & 15)) & 1, 0)
    turn = (2 * HP - p0) & (NP - 1)
    turn = jnp.where(turn > 14, 0, turn)
    col_of = lax.broadcasted_iota(jnp.int32, (BS, BS), 1)
    row_of = lax.broadcasted_iota(jnp.int32, (BS, BS), 0)
    ahead = ((row_of - turn) & 15) < ((col_of - turn) & 15)
    ahead = jnp.where(ahead, 1.0, 0.0).astype(jnp.bfloat16)
    rank = jnp.dot(held.astype(jnp.bfloat16), ahead, preferred_element_type=jnp.float32)
    rank = rank.astype(jnp.int32)
    slot = lax.broadcasted_iota(jnp.int32, (40, BS), 0)
    panels = ((p0 - 2 * HP + lane) & (NP - 1)).astype(jnp.bfloat16)
    slots = lax.broadcasted_iota(jnp.int32, (1, 40), 1)
    start = before
    for r in range(PB):
        taken = (rank[r : r + 1, :] == slot) & (held[r : r + 1, :] > 0)
        taken = jnp.where(taken, 1.0, 0.0).astype(jnp.bfloat16)
        col = lax.dot_general(
            panels, taken, (((1,), (1,)), ((), ())), preferred_element_type=jnp.float32
        )
        cols = jnp.where(slots < count[r : r + 1, :], PB * col[:1].astype(jnp.int32) + c, -1)
        cols_ref[r : r + 1, :] = cols[:, :WIDTH]
        starts_ref[:, r : r + 1] = jnp.broadcast_to(start, (1, 1))
        start = start + count[r : r + 1, :]
    window = lax.broadcasted_iota(jnp.int32, (2 * WIN, NP), 0)
    panels = lax.broadcasted_iota(jnp.int32, (2 * WIN, NP), 1)
    pick = jnp.where(panels == ((p0 - HP + window) & (NP - 1)), 1.0, 0.0).astype(jnp.bfloat16)
    near = lax.dot_general(
        pick,
        turned.astype(jnp.float32).astype(jnp.bfloat16),
        (((1,), (1,)), ((), ())),
        preferred_element_type=jnp.float32,
    )
    map_ref[:WIN, : GROUPS * ROOM] = near[:WIN].astype(jnp.int32)
    map_ref[WIN:, :] = rank


def square_kernel(
    map_ref, up_ref, over_ref, down_ref, trio_ref, swap_ref, back_ref, far_ref, out_ref, *refs
):
    rights, sums, staged, blank, in_sem, zero_sem, out_sem = refs
    p0, c = place()
    core = p0 & 1
    blank[...] = jnp.zeros(blank.shape, blank.dtype)
    for r in range(PB):
        pltpu.make_async_copy(blank, out_ref.at[r, USED:], zero_sem.at[r]).start()
    moves = (
        (trio_ref.at[0], HP, HP),
        (trio_ref.at[1], 2, 2),
        (trio_ref.at[2], 6, 6),
        (swap_ref.at[0], 5, 3),
        (swap_ref.at[1], 3, 1),
        (swap_ref.at[2], 7, 5),
        (back_ref, 0, 0),
        (far_ref, 1, 7),
    )
    copies = []
    for n, (ref, even, odd) in enumerate(moves):
        w = even if even == odd else jnp.where(core == 0, even, odd)
        copies.append(pltpu.make_async_copy(ref, rights.at[w], in_sem.at[n]))
    for copy in copies:
        copy.start()
    sums[...] = jnp.zeros(sums.shape, jnp.float32)
    for copy in copies:
        copy.wait()

    def row_step(r, carry):
        for d in range(GROUPS):
            g = (c + d) & (GROUPS - 1)
            left_ref = (trio_ref.at[0], up_ref, over_ref, down_ref)[d]
            for s0 in range(KG):
                w = map_ref[HP, ROOM * g + KG * r + s0]
                slots = []
                for s in range(KG):
                    slots.append(map_ref[WIN + r, map_ref[w, ROOM * c + KG * g + s] + w])
                right = jnp.concatenate([rights[w, g, s] for s in range(KG)], axis=1)
                product = jnp.dot(left_ref[r, s0], right, preferred_element_type=jnp.float32)
                new = [
                    sums[r, slots[s]] + product[:, BS * s : BS * (s + 1)] for s in range(KG)
                ]
                for s in range(KG):
                    sums[r, slots[s]] = new[s]
        staged[r] = sums[r].astype(jnp.bfloat16)
        pltpu.make_async_copy(staged.at[r], out_ref.at[r, :USED], out_sem.at[r]).start()
        return carry

    lax.fori_loop(0, PB, row_step, 0)
    for r in range(PB):
        pltpu.make_async_copy(blank, out_ref.at[r, USED:], zero_sem.at[r]).wait()
        pltpu.make_async_copy(staged.at[r], out_ref.at[r, :USED], out_sem.at[r]).wait()


VMEM = pl.BlockSpec(memory_space=pltpu.VMEM)
SMEM = pl.BlockSpec(memory_space=pltpu.SMEM)
HBM = pl.BlockSpec(memory_space=pl.ANY)


def near_core(array):
    return pltpu.with_memory_space_constraint(array, pltpu.VMEM)


def spread(cols):
    return pl.pallas_call(
        spread_kernel,
        out_shape=jax.ShapeDtypeStruct((FAR, 1, BS), jnp.int32),
        in_specs=[SMEM],
        out_specs=VMEM,
        compiler_params=pltpu.CompilerParams(vmem_limit_bytes=8 << 20),
        name="spread",
    )(cols)


def turned_table(parts):
    return pl.pallas_call(
        turn_kernel,
        out_shape=jax.ShapeDtypeStruct((NEAR, ROOM, BS), jnp.int32),
        in_specs=[VMEM],
        out_specs=VMEM,
        scratch_shapes=[pltpu.VMEM((NP, BS), jnp.int32)],
        compiler_params=pltpu.CompilerParams(vmem_limit_bytes=8 << 20),
        name="turned_table",
    )(parts)


def indices(table):
    return pl.pallas_call(
        index_kernel,
        out_shape=(
            jax.ShapeDtypeStruct((PB, WIDTH), jnp.int32),
            jax.ShapeDtypeStruct((1, PB), jnp.int32),
            jax.ShapeDtypeStruct((16, BS), jnp.int32),
        ),
        in_specs=[VMEM],
        out_specs=(VMEM, VMEM, VMEM),
        scratch_shapes=[pltpu.VMEM((GROUPS * ROOM, NP), jnp.int32)],
        compiler_params=pltpu.CompilerParams(vmem_limit_bytes=8 << 20),
        name="indices",
    )(table)


def square(where, lefts, pieces):
    return pl.pallas_call(
        square_kernel,
        out_shape=jax.ShapeDtypeStruct((PB, WIDTH, BS, BS), jnp.bfloat16),
        in_specs=[SMEM] + [VMEM] * (len(lefts) + len(pieces)),
        out_specs=HBM,
        scratch_shapes=[
            pltpu.VMEM((WIN, PB, KG, BS, BS), jnp.bfloat16),
            pltpu.VMEM((PB, USED, BS, BS), jnp.float32),
            pltpu.VMEM((PB, USED, BS, BS), jnp.bfloat16),
            pltpu.VMEM((WIDTH - USED, BS, BS), jnp.bfloat16),
            pltpu.SemaphoreType.DMA((WIN,)),
            pltpu.SemaphoreType.DMA((PB,)),
            pltpu.SemaphoreType.DMA((PB,)),
        ],
        compiler_params=pltpu.CompilerParams(vmem_limit_bytes=24 << 20),
        name="square",
    )(where, *[near_core(piece) for piece in (*lefts, *pieces)])


def exchange(array, axes):
    return lax.all_to_all(array, axes, 0, 0, tiled=True)


def swapped(block):
    return lax.ppermute(block, "rows_2", [(0, 1), (1, 0)])


def turned(block, distance):
    return lax.ppermute(block, "cols", [((c + distance) % GROUPS, c) for c in range(GROUPS)])


def sent_on(block, chips, crossed=False):
    count = NP // 2
    route = []
    for q in range(count):
        for core in range(2):
            step = chips * (2 * core - 1) if crossed else chips
            route.append((2 * q + core, 2 * ((q + step) % count) + (core ^ crossed)))
    return lax.ppermute(block, ROWS, route)


def on_device(blocks, block_cols):
    own = blocks[:, 0]
    parts = exchange(spread(block_cols.transpose(2, 1, 0)), FAR_AXES)
    table = exchange(turned_table(parts), NEAR_AXES)
    columns, starts, where = indices(table)
    behind = sent_on(own, 1)
    ahead = sent_on(own, -1)
    far = sent_on(own, 2, True)
    over = turned(own, 2)
    up = turned(own, 1)
    down = turned(own, 3)
    back = sent_on(behind, 1)
    trio = jnp.stack([own, behind, ahead])
    swap = swapped(trio)
    out = square(where, (up, over, down), (trio, swap, back, far))
    return out[:, None], columns[:, None], starts.reshape(PB, 1)


def solution(mesh):
    split = Mesh(
        mesh.devices.reshape(16, 4, 2, mesh.shape["cols"]), ("rows_0", "rows_1", "rows_2", "cols")
    )
    return jax.shard_map(
        on_device,
        mesh=split,
        in_specs=(P(ROWS, "cols", None, None, None), P(ROWS, "cols", None)),
        out_specs=(P(ROWS, "cols", None, None, None), P(ROWS, "cols", None), P(ROWS, "cols")),
        check_vma=False,
    )
```

profile of v0, /device:TPU:1, one launch (start us, length us, event | category | flops | bytes accessed | tf_op | source)
XLA Modules:
  0.0 92.5 jit_solution(18048602715653627082)
XLA Ops:
  0.6 14.4 %collective-permute-start.4 = (bf16[4,3,128,128]{3,2,1,0:T(8,128)(2,1)}, bf16[4,3,128,128]{3,2,1,0:T(8,128)(2,1)S(1)}, u32[]{:S(2)}, u32[]{:S(2)}) collective-permute-start(bf16[4,3,128,128]{3,2,1,0:T(8,128)(2,1)} %bitcast.14), channel_id=1, source_target_pairs={{0,504},{4,508},{8,0},{12,4},{16,8},{20,12},{24,16},{28,20},{32,24... | collective-permute-start | bytes 1179656 | tf_op jit(solution)/shard_map/ppermute | solution.py:272
  15.0 1.9 %collective-permute-start.3 = (bf16[4,3,128,128]{3,2,1,0:T(8,128)(2,1)}, bf16[4,3,128,128]{3,2,1,0:T(8,128)(2,1)S(1)}, u32[]{:S(2)}, u32[]{:S(2)}) collective-permute-start(bf16[4,3,128,128]{3,2,1,0:T(8,128)(2,1)} %bitcast.15), channel_id=1, source_target_pairs={{0,8},{4,12},{8,16},{12,20},{16,24},{20,28},{24,32},{28,36},{32,40... | collective-permute-start | bytes 1179656 | tf_op jit(solution)/shard_map/ppermute | solution.py:272
  17.0 6.2 %collective-permute-done.4 = bf16[4,3,128,128]{3,2,1,0:T(8,128)(2,1)S(1)} collective-permute-done((bf16[4,3,128,128]{3,2,1,0:T(8,128)(2,1)}, bf16[4,3,128,128]{3,2,1,0:T(8,128)(2,1)S(1)}, u32[]{:S(2)}, u32[]{:S(2)}) %collective-permute-start.4) | collective-permute-done | bytes 393248 | tf_op jit(solution)/shard_map/ppermute | solution.py:272
  23.1 7.1 %collective-permute-done.3 = bf16[4,3,128,128]{3,2,1,0:T(8,128)(2,1)S(1)} collective-permute-done((bf16[4,3,128,128]{3,2,1,0:T(8,128)(2,1)}, bf16[4,3,128,128]{3,2,1,0:T(8,128)(2,1)S(1)}, u32[]{:S(2)}, u32[]{:S(2)}) %collective-permute-start.3) | collective-permute-done | bytes 393248 | tf_op jit(solution)/shard_map/ppermute | solution.py:272
  30.2 0.0 copy-start.1
  30.2 0.0 copy-start
  30.2 1.2 %pad_maximum_fusion.trio_ref = bf16[3,4,3,128,128]{4,3,2,1,0:T(8,128)(2,1)S(1)} fusion(bf16[1,4,3,128,128]{4,3,2,1,0:T(8,128)(2,1)S(1)} %bitcast.22, bf16[1,4,3,128,128]{4,3,2,1,0:T(8,128)(2,1)S(1)} %bitcast.21, bf16[1,4,3,128,128]{4,3,2,1,0:T(8,128)(2,1)} %bitcast.16), kind=kLoop, calls=%fused_computation | loop fusion | flops 1179648 | bytes 2359296 | tf_op jit(solution)/shard_map/stack | solution.py:287
  31.4 3.7 %collective-permute-start.5 = (bf16[3,4,3,128,128]{4,3,2,1,0:T(8,128)(2,1)S(1)}, bf16[3,4,3,128,128]{4,3,2,1,0:T(8,128)(2,1)S(1)}, u32[]{:S(2)}, u32[]{:S(2)}) collective-permute-start(bf16[3,4,3,128,128]{4,3,2,1,0:T(8,128)(2,1)S(1)} %pad_maximum_fusion.trio_ref), channel_id=1, source_target_pairs={{0,4},{4,0},{1,5},{5,1},{2,6},{6,2},{3,7},{7,3},{8,12},{12,8},{9,1... | collective-permute-start | bytes 3538952 | tf_op jit(solution)/shard_map/ppermute | solution.py:258
  35.1 0.0 copy-done.1
  35.1 1.9 %collective-permute-start.7 = (bf16[4,3,128,128]{3,2,1,0:T(8,128)(2,1)S(1)}, bf16[4,3,128,128]{3,2,1,0:T(8,128)(2,1)S(1)}, u32[]{:S(2)}, u32[]{:S(2)}) collective-permute-start(bf16[4,3,128,128]{3,2,1,0:T(8,128)(2,1)S(1)} %bitcast.17), channel_id=1, source_target_pairs={{0,500},{4,16},{8,508},{12,24},{16,4},{20,32},{24,12},{28,40},{32,... | collective-permute-start | bytes 1179656 | tf_op jit(solution)/shard_map/ppermute | solution.py:272
  37.0 3.1 %collective-permute-start.2 = (bf16[4,3,128,128]{3,2,1,0:T(8,128)(2,1)S(1)}, bf16[4,3,128,128]{3,2,1,0:T(8,128)(2,1)S(1)}, u32[]{:S(2)}, u32[]{:S(2)}) collective-permute-start(bf16[4,3,128,128]{3,2,1,0:T(8,128)(2,1)S(1)} %bitcast.18), channel_id=1, source_target_pairs={{3,0},{0,1},{1,2},{2,3},{7,4},{4,5},{5,6},{6,7},{11,8},{8,9},{9,10... | collective-permute-start | bytes 1179656 | tf_op jit(solution)/shard_map/ppermute | solution.py:262
  40.2 4.4 %collective-permute-start.1 = (bf16[4,3,128,128]{3,2,1,0:T(8,128)(2,1)S(1)}, bf16[4,3,128,128]{3,2,1,0:T(8,128)(2,1)S(1)}, u32[]{:S(2)}, u32[]{:S(2)}) collective-permute-start(bf16[4,3,128,128]{3,2,1,0:T(8,128)(2,1)S(1)} %bitcast.19), channel_id=1, source_target_pairs={{2,0},{3,1},{0,2},{1,3},{6,4},{7,5},{4,6},{5,7},{10,8},{11,9},{8,1... | collective-permute-start | bytes 1179656 | tf_op jit(solution)/shard_map/ppermute | solution.py:262
  44.5 3.1 %collective-permute-start = (bf16[4,3,128,128]{3,2,1,0:T(8,128)(2,1)S(1)}, bf16[4,3,128,128]{3,2,1,0:T(8,128)(2,1)S(1)}, u32[]{:S(2)}, u32[]{:S(2)}) collective-permute-start(bf16[4,3,128,128]{3,2,1,0:T(8,128)(2,1)S(1)} %bitcast.20), channel_id=1, source_target_pairs={{1,0},{2,1},{3,2},{0,3},{5,4},{6,5},{7,6},{4,7},{9,8},{10,9},{11,1... | collective-permute-start | bytes 1179656 | tf_op jit(solution)/shard_map/ppermute | solution.py:262
  47.6 5.3 %collective-permute-done.7.far_ref = bf16[4,3,128,128]{3,2,1,0:T(8,128)(2,1)S(1)} collective-permute-done((bf16[4,3,128,128]{3,2,1,0:T(8,128)(2,1)S(1)}, bf16[4,3,128,128]{3,2,1,0:T(8,128)(2,1)S(1)}, u32[]{:S(2)}, u32[]{:S(2)}) %collective-permute-start.7) | collective-permute-done | bytes 393248 | tf_op jit(solution)/shard_map/ppermute | solution.py:272
  52.9 1.9 %collective-permute-start.6 = (bf16[4,3,128,128]{3,2,1,0:T(8,128)(2,1)S(1)}, bf16[4,3,128,128]{3,2,1,0:T(8,128)(2,1)S(1)}, u32[]{:S(2)}, u32[]{:S(2)}) collective-permute-start(bf16[4,3,128,128]{3,2,1,0:T(8,128)(2,1)S(1)} %collective-permute-done.3), channel_id=1, source_target_pairs={{0,8},{4,12},{8,16},{12,20},{16,24},{20,28},{24,32},{28,36},{32,40... | collective-permute-start | bytes 1179656 | tf_op jit(solution)/shard_map/ppermute | solution.py:272
  54.8 0.0 copy-done
  54.8 0.6 spread.1
  55.4 14.6 %all_to_all.10.in_ref = s32[32,1,128]{2,1,0:T(1,128)S(1)} all-to-all(s32[32,1,128]{2,1,0:T(1,128)S(1)} %spread.1), channel_id=1, replica_groups=mesh['rows_0'=16,'rows_1'=4,'rows_2'=2,'cols'=4] {'rows_0','rows_2'}, dimensions={0} | all-to-all | bytes 32768 | tf_op jit(solution)/shard_map/all_to_all | solution.py:254
  70.0 0.1 turned_table.1
  70.1 15.5 %all_to_all.11.tab_ref = s32[16,16,128]{2,1,0:T(8,128)S(1)} all-to-all(s32[16,16,128]{2,1,0:T(8,128)S(1)} %turned_table.1), channel_id=1, replica_groups=mesh['rows_0'=16,'rows_1'=4,'rows_2'=2,'cols'=4] {'rows_1','cols'}, dimensions={0} | all-to-all | bytes 262144 | tf_op jit(solution)/shard_map/all_to_all | solution.py:254
  85.6 1.1 %indices.1 = (s32[4,36]{1,0:T(4,128)}, s32[1,4]{1,0:T(1,128)}, s32[16,128]{1,0:T(8,128)S(1)}) custom-call(s32[16,16,128]{2,1,0:T(8,128)S(1)} %all_to_all.11.tab_ref), custom_call_target="tpu_custom_call" | custom-call | tf_op jit(solution)/shard_map/indices/pallas_call | solution.py:218
  86.7 0.0 collective-permute-done.2.down_ref
  86.7 0.0 collective-permute-done.1.over_ref
  86.7 0.0 collective-permute-done.up_ref
  86.7 0.0 collective-permute-done.6.back_ref
  86.8 0.0 collective-permute-done.5.swap_ref
  86.8 5.7 %square.1 = bf16[4,36,128,128]{3,2,1,0:T(8,128)(2,1)} custom-call(s32[16,128]{1,0:T(8,128)S(1)} %get-tuple-element.6.map_ref, bf16[4,3,128,128]{3,2,1,0:T(8,128)(2,1)S(1)} %collective-permute-done.up_ref, bf16[4,3,128,128]{3,2,1,0:T(8,128)(2,1)S(1)} %collective-permute-done.1.over_ref, bf16[4,3,128,128]{3,2,1,0:T(8,128)(2,1)S(1)} %collective-permute-done.2.down_ref, ...), custom_call_target="tpu_custom_call" | custom-call | tf_op jit(solution)/shard_map/square/pallas_call | solution.py:234
Async XLA Ops:
  0.6 22.5 %collective-permute-start.4 = (bf16[4,3,128,128]{3,2,1,0:T(8,128)(2,1)}, bf16[4,3,128,128]{3,2,1,0:T(8,128)(2,1)S(1)}, u32[]{:S(2)}, u32[]{:S(2)}) collective-permute-start(bf16[4,3,128,128]{3,2,1,0:T(8,128)(2,1)} %bitcast.14), channel_id=1, source_target_pairs={{0,504},{4,508},{8,0},{12,4},{16,8},{20,12},{24,16},{28,20},{32,24... | collective-permute-start | bytes 1179656 | tf_op jit(solution)/shard_map/ppermute | solution.py:272
  15.0 15.1 %collective-permute-start.3 = (bf16[4,3,128,128]{3,2,1,0:T(8,128)(2,1)}, bf16[4,3,128,128]{3,2,1,0:T(8,128)(2,1)S(1)}, u32[]{:S(2)}, u32[]{:S(2)}) collective-permute-start(bf16[4,3,128,128]{3,2,1,0:T(8,128)(2,1)} %bitcast.15), channel_id=1, source_target_pairs={{0,8},{4,12},{8,16},{12,20},{16,24},{20,28},{24,32},{28,36},{32,40... | collective-permute-start | bytes 1179656 | tf_op jit(solution)/shard_map/ppermute | solution.py:272
  30.2 4.9 %copy-start.1 = (bf16[4,1,3,128,128]{4,3,2,1,0:T(8,128)(2,1)S(1)}, bf16[4,1,3,128,128]{4,3,2,1,0:T(8,128)(2,1)}, u32[]{:S(2)}) copy-start(bf16[4,1,3,128,128]{4,3,2,1,0:T(8,128)(2,1)} %param.2) | copy-start | bytes 1179652
  30.2 24.6 %copy-start = (s32[4,1,3]{0,1,2:T(1,128)S(1)}, s32[4,1,3]{0,1,2:T(1,128)}, u32[]{:S(2)}) copy-start(s32[4,1,3]{0,1,2:T(1,128)} %param.3) | copy-start | bytes 148
  31.4 55.4 %collective-permute-start.5 = (bf16[3,4,3,128,128]{4,3,2,1,0:T(8,128)(2,1)S(1)}, bf16[3,4,3,128,128]{4,3,2,1,0:T(8,128)(2,1)S(1)}, u32[]{:S(2)}, u32[]{:S(2)}) collective-permute-start(bf16[3,4,3,128,128]{4,3,2,1,0:T(8,128)(2,1)S(1)} %pad_maximum_fusion.trio_ref), channel_id=1, source_target_pairs={{0,4},{4,0},{1,5},{5,1},{2,6},{6,2},{3,7},{7,3},{8,12},{12,8},{9,1... | collective-permute-start | bytes 3538952 | tf_op jit(solution)/shard_map/ppermute | solution.py:258
  35.1 17.8 %collective-permute-start.7 = (bf16[4,3,128,128]{3,2,1,0:T(8,128)(2,1)S(1)}, bf16[4,3,128,128]{3,2,1,0:T(8,128)(2,1)S(1)}, u32[]{:S(2)}, u32[]{:S(2)}) collective-permute-start(bf16[4,3,128,128]{3,2,1,0:T(8,128)(2,1)S(1)} %bitcast.17), channel_id=1, source_target_pairs={{0,500},{4,16},{8,508},{12,24},{16,4},{20,32},{24,12},{28,40},{32,... | collective-permute-start | bytes 1179656 | tf_op jit(solution)/shard_map/ppermute | solution.py:272
  37.0 49.7 %collective-permute-start.2 = (bf16[4,3,128,128]{3,2,1,0:T(8,128)(2,1)S(1)}, bf16[4,3,128,128]{3,2,1,0:T(8,128)(2,1)S(1)}, u32[]{:S(2)}, u32[]{:S(2)}) collective-permute-start(bf16[4,3,128,128]{3,2,1,0:T(8,128)(2,1)S(1)} %bitcast.18), channel_id=1, source_target_pairs={{3,0},{0,1},{1,2},{2,3},{7,4},{4,5},{5,6},{6,7},{11,8},{8,9},{9,10... | collective-permute-start | bytes 1179656 | tf_op jit(solution)/shard_map/ppermute | solution.py:262
  40.2 46.6 %collective-permute-start.1 = (bf16[4,3,128,128]{3,2,1,0:T(8,128)(2,1)S(1)}, bf16[4,3,128,128]{3,2,1,0:T(8,128)(2,1)S(1)}, u32[]{:S(2)}, u32[]{:S(2)}) collective-permute-start(bf16[4,3,128,128]{3,2,1,0:T(8,128)(2,1)S(1)} %bitcast.19), channel_id=1, source_target_pairs={{2,0},{3,1},{0,2},{1,3},{6,4},{7,5},{4,6},{5,7},{10,8},{11,9},{8,1... | collective-permute-start | bytes 1179656 | tf_op jit(solution)/shard_map/ppermute | solution.py:262
  44.5 42.2 %collective-permute-start = (bf16[4,3,128,128]{3,2,1,0:T(8,128)(2,1)S(1)}, bf16[4,3,128,128]{3,2,1,0:T(8,128)(2,1)S(1)}, u32[]{:S(2)}, u32[]{:S(2)}) collective-permute-start(bf16[4,3,128,128]{3,2,1,0:T(8,128)(2,1)S(1)} %bitcast.20), channel_id=1, source_target_pairs={{1,0},{2,1},{3,2},{0,3},{5,4},{6,5},{7,6},{4,7},{9,8},{10,9},{11,1... | collective-permute-start | bytes 1179656 | tf_op jit(solution)/shard_map/ppermute | solution.py:262
  52.9 33.9 %collective-permute-start.6 = (bf16[4,3,128,128]{3,2,1,0:T(8,128)(2,1)S(1)}, bf16[4,3,128,128]{3,2,1,0:T(8,128)(2,1)S(1)}, u32[]{:S(2)}, u32[]{:S(2)}) collective-permute-start(bf16[4,3,128,128]{3,2,1,0:T(8,128)(2,1)S(1)} %collective-permute-done.3), channel_id=1, source_target_pairs={{0,8},{4,12},{8,16},{12,20},{16,24},{20,28},{24,32},{28,36},{32,40... | collective-permute-start | bytes 1179656 | tf_op jit(solution)/shard_map/ppermute | solution.py:272
where the time goes:
time: 92.9 us; the launch traced here: 92.5 us
  starting transfers between devices  34.4 us (37%)
  blocking collectives  30.2 us (33%)
  waiting for transfers between devices  18.5 us (20%)
  Pallas kernels  7.44 us (8%)
  other arithmetic  1.19 us (1%)
    all_to_all x2, blocking collectives, exchange(): return lax.all_to_all(array, axes, 0, 0, tiled=True)  30.2 us
    ppermute x4, starting transfers between devices, sent_on(): return lax.ppermute(block, ROWS, route)  20.1 us
    ppermute x4, waiting for transfers between devices, sent_on(): return lax.ppermute(block, ROWS, route)  18.5 us
    ppermute x3, starting transfers between devices, turned(): lax.ppermute(block, 'cols', [((c + distance) % GROUPS, c) for c in range(...  10.5 us
    pallas_call x1, Pallas kernels, square(): pl.pallas_call(square_kernel, out_shape=jax.ShapeDtypeStruct((PB, WIDTH,...  5.7 us
    ppermute x1, starting transfers between devices, swapped(): return lax.ppermute(block, 'rows_2', [(0, 1), (1, 0)])  3.72 us
  transfers between devices with their start and end apart: 8, of which 3 were waited for; matrix products, arithmetic and copies ran while one was open for 0% of the time, Pallas kernels for 2%

commit v1 on v0

v1 whole, which is shorter than its diff:
```python
import jax
import jax.numpy as jnp
from jax import lax
from jax.experimental import pallas as pl
from jax.experimental.pallas import tpu as pltpu
from jax.sharding import Mesh
from jax.sharding import PartitionSpec as P

HP = 4
PB = 4
KG = 3
GROUPS = 4
BS = 128
NP = 128
WIDTH = 36
USED = 15
WIN = 2 * HP
ROOM = 16
FULL = PB * KG * BS
LONG = FULL + ROOM
ROWS = ("rows_0", "rows_1", "rows_2")


def place():
    return lax.axis_index(ROWS), lax.axis_index("cols")


def spread_kernel(in_ref, out_ref):
    lane = lax.broadcasted_iota(jnp.int32, (1, BS), 1)
    row = jnp.zeros((1, BS), jnp.float32)
    for g in range(GROUPS):
        part = in_ref[g].astype(jnp.float32)[:1]
        row = row + pltpu.roll(jnp.where(lane < PB * KG, part, 0.0), ROOM * g, 1)
    out_ref[...] = jnp.broadcast_to(row.astype(jnp.int32)[None], out_ref.shape)


def bits_set(x):
    x = x - ((x >> 1) & 0x5555)
    x = (x & 0x3333) + ((x >> 2) & 0x3333)
    x = (x + (x >> 4)) & 0x0F0F
    return (x + (x >> 8)) & 0x1F


def starts_kernel(tab_ref, starts_ref, table_ref, turned_ref):
    p0, c = place()
    for n in range(NP):
        table_ref[n : n + 1, :] = tab_ref[n]
    panel = lax.broadcasted_iota(jnp.int32, (1, NP), 1)
    turned_ref[...] = (jnp.transpose(table_ref[...]) - panel + HP) & (NP - 1)
    wants = []
    owns = []
    for r in range(PB):
        want = jnp.zeros((1, NP), jnp.int32)
        for g in range(GROUPS):
            for s in range(KG):
                at = ROOM * g + KG * r + s
                want = want | jnp.left_shift(1, PB * turned_ref[at : at + 1, :] + g)
        wants.append(want)
        own = jnp.zeros((1, NP), jnp.int32)
        for s in range(KG):
            own = own | jnp.left_shift(1, turned_ref[pl.ds(ROOM * c + KG * r + s, 1), :])
        owns.append(own)
    pad = [jnp.zeros((PB, NP), jnp.int32)]
    want = jnp.concatenate(wants + pad, axis=0)
    own = jnp.concatenate(owns + pad, axis=0)
    found = jnp.zeros((8, NP), jnp.int32)
    for w in range(WIN):
        there = pltpu.roll(own, (HP - w) % NP, 1) if w != HP else own
        there = there << w
        for kr in range(PB):
            used = -((want >> (PB * w + kr)) & 1)
            found = found | (used & there[kr : kr + 1, :])
    counts = bits_set(found)
    before = jnp.sum(jnp.where(panel < p0, counts, 0).astype(jnp.float32)).astype(jnp.int32)
    here = jnp.where(panel == p0, 1, 0)
    count = jnp.sum((counts * here).astype(jnp.float32), axis=1, keepdims=True).astype(jnp.int32)
    start = before
    for r in range(PB):
        starts_ref[:, r : r + 1] = jnp.broadcast_to(start, (1, 1))
        start = start + count[r : r + 1, :]


def find_slots(lefts, rights, cols_ref, map_ref):
    p0, c = place()
    side = lax.broadcasted_iota(jnp.int32, (WIN, 1), 0)
    there = [rights[w, FULL:LONG].astype(jnp.float32)[:1] for w in range(WIN)]
    there = jnp.concatenate(there, axis=0).astype(jnp.int32)
    there = (there - (p0 + side) + 2 * HP) & (NP - 1)
    here = [lefts[g, FULL:LONG].astype(jnp.float32)[:1] for g in range(GROUPS)]
    here = jnp.concatenate(here + here, axis=0).astype(jnp.int32)
    here = (here - p0 + HP) & (NP - 1)
    map_ref[:WIN] = there
    map_ref[WIN : WIN + PB] = here[:GROUPS]
    group = lax.broadcasted_iota(jnp.int32, (WIN, 1), 0) & (GROUPS - 1)
    want_bits = jnp.left_shift(1, (PB * here + group) & 31)
    want_bits = want_bits[:1] | want_bits[1:2] | want_bits[2:3] | want_bits[3:4]
    own_bits = jnp.left_shift(1, there & 31)
    rows = []
    for r in range(PB):
        want = jnp.zeros((1, 1), jnp.int32)
        for s in range(KG):
            want = want | want_bits[:, KG * r + s : KG * r + s + 1]
        found = jnp.zeros((WIN, 1), jnp.int32)
        for kr in range(PB):
            own = jnp.zeros((WIN, 1), jnp.int32)
            for s in range(KG):
                own = own | own_bits[:, KG * kr + s : KG * kr + s + 1]
            used = -((want >> (PB * side + kr)) & 1)
            found = found | (used & (own << side))
        found = found[:4] | found[4:]
        found = found[:2] | found[2:]
        rows.append(found[:1] | found[1:])
    mask = jnp.concatenate(rows + rows, axis=0)
    count = bits_set(mask)
    lane = lax.broadcasted_iota(jnp.int32, (8, BS), 1)
    held = jnp.where(lane < 16, (jnp.broadcast_to(mask, (8, BS)) >> (lane & 15)) & 1, 0)
    turn = (2 * HP - p0) & (NP - 1)
    turn = jnp.where(turn > 14, 0, turn)
    col_of = lax.broadcasted_iota(jnp.int32, (BS, BS), 1)
    row_of = lax.broadcasted_iota(jnp.int32, (BS, BS), 0)
    ahead = ((row_of - turn) & 15) < ((col_of - turn) & 15)
    ahead = jnp.where(ahead, 1.0, 0.0).astype(jnp.bfloat16)
    rank = jnp.dot(
        held.astype(jnp.float32).astype(jnp.bfloat16), ahead, preferred_element_type=jnp.float32
    )
    rank = rank.astype(jnp.int32)
    map_ref[WIN + PB :] = rank[:PB]
    slot = lax.broadcasted_iota(jnp.int32, (40, BS), 0)
    panels = ((p0 - 2 * HP + lane) & (NP - 1)).astype(jnp.float32).astype(jnp.bfloat16)
    slots = lax.broadcasted_iota(jnp.int32, (1, 40), 1)
    for r in range(PB):
        taken = (rank[r : r + 1, :] == slot) & (held[r : r + 1, :] > 0)
        taken = jnp.where(taken, 1.0, 0.0).astype(jnp.bfloat16)
        col = lax.dot_general(
            panels, taken, (((1,), (1,)), ((), ())), preferred_element_type=jnp.float32
        )
        cols = jnp.where(slots < count[r : r + 1, :], PB * col[:1].astype(jnp.int32) + c, -1)
        cols_ref[r : r + 1, :] = cols[:, :WIDTH]


def square_kernel(
    lefts, trio_ref, swap_ref, back_ref, far_ref, out_ref, cols_ref, *refs
):
    rights, sums, staged, blank, found, map_ref, map_sem, in_sem, zero_sem, out_sem = refs
    p0, _ = place()
    core = p0 & 1
    blank[...] = jnp.zeros(blank.shape, blank.dtype)
    for r in range(PB):
        pltpu.make_async_copy(blank, out_ref.at[r, USED:], zero_sem.at[r]).start()
    moves = (
        (trio_ref.at[0], HP, HP),
        (trio_ref.at[1], 2, 2),
        (trio_ref.at[2], 6, 6),
        (swap_ref.at[0], 5, 3),
        (swap_ref.at[1], 3, 1),
        (swap_ref.at[2], 7, 5),
        (back_ref, 0, 0),
        (far_ref, 1, 7),
    )
    copies = []
    for n, (ref, even, odd) in enumerate(moves):
        w = even if even == odd else jnp.where(core == 0, even, odd)
        copies.append(pltpu.make_async_copy(ref, rights.at[w], in_sem.at[n]))
    for copy in copies:
        copy.start()
    for copy in copies:
        copy.wait()
    find_slots(lefts, rights, cols_ref, found)
    told = pltpu.make_async_copy(found, map_ref, map_sem)
    told.start()
    sums[...] = jnp.zeros(sums.shape, jnp.float32)
    told.wait()

    def row_step(r, carry):
        for g in range(GROUPS):
            for s0 in range(KG):
                w = map_ref[WIN + g, KG * r + s0]
                slots = []
                right = []
                for s in range(KG):
                    slots.append(map_ref[WIN + PB + r, map_ref[w, KG * g + s] + w])
                    right.append(rights[w, BS * (KG * g + s) : BS * (KG * g + s + 1)])
                right = jnp.concatenate(right, axis=1)
                left = lefts[g, pl.ds(pl.multiple_of(BS * (KG * r + s0), BS), BS)]
                product = jnp.dot(left, right, preferred_element_type=jnp.float32)
                new = [
                    sums[r, slots[s]] + product[:, BS * s : BS * (s + 1)] for s in range(KG)
                ]
                for s in range(KG):
                    sums[r, slots[s]] = new[s]
        staged[r] = sums[r].astype(jnp.bfloat16)
        pltpu.make_async_copy(staged.at[r], out_ref.at[r, :USED], out_sem.at[r]).start()
        return carry

    lax.fori_loop(0, PB, row_step, 0)
    for r in range(PB):
        pltpu.make_async_copy(blank, out_ref.at[r, USED:], zero_sem.at[r]).wait()
        pltpu.make_async_copy(staged.at[r], out_ref.at[r, :USED], out_sem.at[r]).wait()


VMEM = pl.BlockSpec(memory_space=pltpu.VMEM)
SMEM = pl.BlockSpec(memory_space=pltpu.SMEM)
HBM = pl.BlockSpec(memory_space=pl.ANY)


def near_core(array):
    return pltpu.with_memory_space_constraint(array, pltpu.VMEM)


def spread(parts):
    return pl.pallas_call(
        spread_kernel,
        out_shape=jax.ShapeDtypeStruct((NP, 1, BS), jnp.int32),
        in_specs=[VMEM],
        out_specs=VMEM,
        compiler_params=pltpu.CompilerParams(vmem_limit_bytes=8 << 20),
        name="spread",
    )(parts)


def starts_of(table):
    return pl.pallas_call(
        starts_kernel,
        out_shape=jax.ShapeDtypeStruct((1, PB), jnp.int32),
        in_specs=[VMEM],
        out_specs=VMEM,
        scratch_shapes=[pltpu.VMEM((NP, BS), jnp.int32), pltpu.VMEM((BS, NP), jnp.int32)],
        compiler_params=pltpu.CompilerParams(vmem_limit_bytes=8 << 20),
        name="starts",
    )(table)


def square(left, pieces):
    return pl.pallas_call(
        square_kernel,
        out_shape=(
            jax.ShapeDtypeStruct((PB, WIDTH, BS, BS), jnp.bfloat16),
            jax.ShapeDtypeStruct((PB, WIDTH), jnp.int32),
        ),
        in_specs=[VMEM] * (1 + len(pieces)),
        out_specs=(HBM, VMEM),
        scratch_shapes=[
            pltpu.VMEM((WIN, LONG, BS), jnp.bfloat16),
            pltpu.VMEM((PB, USED, BS, BS), jnp.float32),
            pltpu.VMEM((PB, USED, BS, BS), jnp.bfloat16),
            pltpu.VMEM((WIDTH - USED, BS, BS), jnp.bfloat16),
            pltpu.VMEM((2 * WIN, BS), jnp.int32),
            pltpu.SMEM((2 * WIN, BS), jnp.int32),
            pltpu.SemaphoreType.DMA,
            pltpu.SemaphoreType.DMA((WIN,)),
            pltpu.SemaphoreType.DMA((PB,)),
            pltpu.SemaphoreType.DMA((PB,)),
        ],
        compiler_params=pltpu.CompilerParams(vmem_limit_bytes=24 << 20),
        name="square",
    )(near_core(left), *[near_core(piece) for piece in pieces])


def exchange(array, axes):
    return lax.all_to_all(array, axes, 0, 0, tiled=True)


def swapped(block):
    return lax.ppermute(block, "rows_2", [(0, 1), (1, 0)])


def sent_on(block, chips, crossed=False):
    count = NP // 2
    route = []
    for q in range(count):
        for core in range(2):
            step = chips * (2 * core - 1) if crossed else chips
            route.append((2 * q + core, 2 * ((q + step) % count) + (core ^ crossed)))
    return lax.ppermute(block, ROWS, route)


def on_device(blocks, block_cols):
    tail = (block_cols.reshape(1, PB * KG) >> 2).astype(jnp.bfloat16)
    tail = jnp.pad(tail, ((0, ROOM - 1), (0, BS - PB * KG)))
    own = jnp.concatenate([blocks.reshape(FULL, BS), tail], axis=0)
    behind = sent_on(own, 1)
    left = exchange(jnp.broadcast_to(own[None], (GROUPS, LONG, BS)), "cols")
    far = sent_on(own, 2, True)
    ahead = sent_on(own, -1)
    back = sent_on(behind, 1)
    trio = jnp.stack([own, behind, ahead])
    swap = swapped(trio)
    table = exchange(spread(left[:, FULL:]), ROWS)
    starts = starts_of(table)
    out, columns = square(left, (trio, swap, back, far))
    return out[:, None], columns[:, None], starts.reshape(PB, 1)


def solution(mesh):
    split = Mesh(
        mesh.devices.reshape(16, 4, 2, mesh.shape["cols"]), ("rows_0", "rows_1", "rows_2", "cols")
    )
    return jax.shard_map(
        on_device,
        mesh=split,
        in_specs=(P(ROWS, "cols", None, None, None), P(ROWS, "cols", None)),
        out_specs=(P(ROWS, "cols", None, None, None), P(ROWS, "cols", None), P(ROWS, "cols")),
        check_vma=False,
    )
```

time: 92.9 us -> 81.9 us (0.88)
  waiting for transfers between devices: 18.5 us -> 10.5 us
  starting transfers between devices: 34.4 us -> 27.6 us
  blocking collectives: 30.2 us -> 26.3 us
  local copies, waits for them, and re-layouts: 0.01 us -> 3.29 us
  other arithmetic: 1.19 us -> 3.81 us
  Pallas kernels: 7.44 us -> 9.23 us
    ppermute x4, waiting for transfers between devices: 18.5 us -> 1.81 us  [sent_on(): return lax.ppermute(block, ROWS, route)]
    ppermute x3 -> x0, starting transfers between devices: 10.5 us -> none  [turned(): lax.ppermute(block, 'cols', [((c + distance) % GROUPS, c) for c in range(...]
    all_to_all x0 -> x1, waiting for transfers between devices: none -> 8.65 us  [exchange(): return lax.all_to_all(array, axes, 0, 0, tiled=True)]
    all_to_all x0 -> x1, starting transfers between devices: none -> 4.01 us  [exchange(): return lax.all_to_all(array, axes, 0, 0, tiled=True)]
    all_to_all x2 -> x1, blocking collectives: 30.2 us -> 26.3 us  [exchange(): return lax.all_to_all(array, axes, 0, 0, tiled=True)]
    broadcast_in_dim x0 -> x1, local copies, waits for them, and re-layouts: none -> 2.36 us  [on_device(): left = exchange(jnp.broadcast_to(own[None], (GROUPS, LONG, BS)), 'cols')]
    broadcast_in_dim x0 -> x1, other arithmetic: none -> 1.88 us  [on_device(): left = exchange(jnp.broadcast_to(own[None], (GROUPS, LONG, BS)), 'cols')]
    pallas_call x4 -> x3, Pallas kernels: 7.44 us -> 9.23 us  [the longest x1 8.19 us: square(): pl.pallas_call(square_kernel, out_shape=(jax.ShapeDtypeStruct((PB, WIDTH,...]
  transfers between devices with their start and end apart: 8 -> 6, of which waited for: 3 -> 3; matrix products, arithmetic and copies ran while one was open for 0% -> 4% of each run, Pallas kernels for 2% -> 1%
where the time goes in v1:
time: 81.9 us; the launch traced here: 81.4 us
  starting transfers between devices  27.6 us (34%)
  blocking collectives  26.3 us (32%)
  waiting for transfers between devices  10.5 us (13%)
  Pallas kernels  9.23 us (11%)
  other arithmetic  3.81 us (5%)
  local copies, waits for them, and re-layouts  3.29 us (4%)
    all_to_all x1, blocking collectives, exchange(): return lax.all_to_all(array, axes, 0, 0, tiled=True)  26.3 us
    ppermute x4, starting transfers between devices, sent_on(): return lax.ppermute(block, ROWS, route)  20.1 us
    all_to_all x1, waiting for transfers between devices, exchange(): return lax.all_to_all(array, axes, 0, 0, tiled=True)  8.65 us
    pallas_call x1, Pallas kernels, square(): pl.pallas_call(square_kernel, out_shape=(jax.ShapeDtypeStruct((PB, WIDTH,...  8.19 us
    all_to_all x1, starting transfers between devices, exchange(): return lax.all_to_all(array, axes, 0, 0, tiled=True)  4.01 us
    ppermute x1, starting transfers between devices, swapped(): return lax.ppermute(block, 'rows_2', [(0, 1), (1, 0)])  3.44 us
    broadcast_in_dim x1, local copies, waits for them, and re-layouts, on_device(): left = exchange(jnp.broadcast_to(own[None], (GROUPS, LONG, BS)), 'cols')  2.36 us
    broadcast_in_dim x1, other arithmetic, on_device(): left = exchange(jnp.broadcast_to(own[None], (GROUPS, LONG, BS)), 'cols')  1.88 us
  transfers between devices with their start and end apart: 6, of which 3 were waited for; matrix products, arithmetic and copies ran while one was open for 4% of the time, Pallas kernels for 1%

profile of v1, /device:TPU:1, one launch (start us, length us, event | category | flops | bytes accessed | tf_op | source)
XLA Modules:
  0.0 81.4 jit_solution(35416514633741228)
XLA Ops:
  0.6 0.7 shift-right-arithmetic_convert_fusion
  1.3 0.1 copy.5
  1.4 0.1 convert_element_type.17
  1.5 1.9 %fusion.2 = (bf16[1,1552,128]{2,1,0:T(8,128)(2,1)S(1)}, bf16[1552,128]{1,0:T(8,128)(2,1)}) fusion(bf16[1,12]{1,0:T(2,128)(2,1)S(1)} %convert_element_type.17, bf16[1536,128]{1,0:T(8,128)(2,1)} %bitcast.15), kind=kLoop, calls=%fused_computation.5 | loop fusion | flops 1191936 | bytes 1187864 | tf_op jit(solution)/shard_map/broadcast_in_dim | solution.py:282
  3.4 4.0 %collective-permute-start = (bf16[1552,128]{1,0:T(8,128)(2,1)}, bf16[1552,128]{1,0:T(8,128)(2,1)}, u32[]{:S(2)}, u32[]{:S(2)}) collective-permute-start(bf16[1552,128]{1,0:T(8,128)(2,1)} %get-tuple-element.11), channel_id=1, source_target_pairs={{0,8},{4,12},{8,16},{12,20},{16,24},{20,28},{24,32},{28,36},{32,40... | collective-permute-start | bytes 1191944 | tf_op jit(solution)/shard_map/ppermute | solution.py:274
  7.4 12.3 %collective-permute-start.1 = (bf16[1552,128]{1,0:T(8,128)(2,1)}, bf16[1552,128]{1,0:T(8,128)(2,1)S(1)}, u32[]{:S(2)}, u32[]{:S(2)}) collective-permute-start(bf16[1552,128]{1,0:T(8,128)(2,1)} %get-tuple-element.11), channel_id=1, source_target_pairs={{0,504},{4,508},{8,0},{12,4},{16,8},{20,12},{24,16},{28,20},{32,24... | collective-permute-start | bytes 1191944 | tf_op jit(solution)/shard_map/ppermute | solution.py:274
  19.7 2.4 %broadcast_in_dim.14 = bf16[4,1552,128]{2,1,0:T(8,128)(2,1)} broadcast(bf16[1552,128]{1,0:T(8,128)(2,1)} %get-tuple-element.11), dimensions={1,2} | broadcast | bytes 1986560 | tf_op jit(solution)/shard_map/broadcast_in_dim | solution.py:282
  22.1 4.0 %all-to-all-start = ((bf16[4,1552,128]{2,1,0:T(8,128)(2,1)}), bf16[4,1552,128]{2,1,0:T(8,128)(2,1)S(1)}, u32[]{:S(2)}, u32[]{:S(2)}) async-start(bf16[4,1552,128]{2,1,0:T(8,128)(2,1)} %broadcast_in_dim.14), calls=%async_computation | async-start | bytes 3178496 | tf_op jit(solution)/shard_map/all_to_all | solution.py:260
  26.1 0.9 %collective-permute-done = bf16[1552,128]{1,0:T(8,128)(2,1)} collective-permute-done((bf16[1552,128]{1,0:T(8,128)(2,1)}, bf16[1552,128]{1,0:T(8,128)(2,1)}, u32[]{:S(2)}, u32[]{:S(2)}) %collective-permute-start) | collective-permute-done | bytes 397344 | tf_op jit(solution)/shard_map/ppermute | solution.py:274
  27.0 0.9 %collective-permute-done.1 = bf16[1552,128]{1,0:T(8,128)(2,1)S(1)} collective-permute-done((bf16[1552,128]{1,0:T(8,128)(2,1)}, bf16[1552,128]{1,0:T(8,128)(2,1)S(1)}, u32[]{:S(2)}, u32[]{:S(2)}) %collective-permute-start.1) | collective-permute-done | bytes 397344 | tf_op jit(solution)/shard_map/ppermute | solution.py:274
  27.9 0.0 copy-start
  27.9 0.7 copy-done
  28.6 1.2 %pad_maximum_fusion.trio_ref = bf16[3,1552,128]{2,1,0:T(8,128)(2,1)S(1)} fusion(bf16[1,1552,128]{2,1,0:T(8,128)(2,1)} %bitcast.14, bf16[1,1552,128]{2,1,0:T(8,128)(2,1)} %bitcast.2, bf16[1,1552,128]{2,1,0:T(8,128)(2,1)S(1)} %get-tuple-element.10), kind=kLoop, calls=%fused_computation | loop fusion | flops 1191936 | bytes 2383872 | tf_op jit(solution)/shard_map/stack | solution.py:286
  29.9 3.4 %collective-permute-start.2 = (bf16[3,1552,128]{2,1,0:T(8,128)(2,1)S(1)}, bf16[3,1552,128]{2,1,0:T(8,128)(2,1)}, u32[]{:S(2)}, u32[]{:S(2)}) collective-permute-start(bf16[3,1552,128]{2,1,0:T(8,128)(2,1)S(1)} %pad_maximum_fusion.trio_ref), channel_id=1, source_target_pairs={{0,4},{4,0},{1,5},{5,1},{2,6},{6,2},{3,7},{7,3},{8,12},{12,8},{9,1... | collective-permute-start | bytes 3575816 | tf_op jit(solution)/shard_map/ppermute | solution.py:264
  33.3 1.9 %collective-permute-start.4 = (bf16[1552,128]{1,0:T(8,128)(2,1)}, bf16[1552,128]{1,0:T(8,128)(2,1)S(1)}, u32[]{:S(2)}, u32[]{:S(2)}) collective-permute-start(bf16[1552,128]{1,0:T(8,128)(2,1)} %get-tuple-element.11), channel_id=1, source_target_pairs={{0,500},{4,16},{8,508},{12,24},{16,4},{20,32},{24,12},{28,40},{32,... | collective-permute-start | bytes 1191944 | tf_op jit(solution)/shard_map/ppermute | solution.py:274
  35.2 1.9 %collective-permute-start.3 = (bf16[1552,128]{1,0:T(8,128)(2,1)}, bf16[1552,128]{1,0:T(8,128)(2,1)}, u32[]{:S(2)}, u32[]{:S(2)}) collective-permute-start(bf16[1552,128]{1,0:T(8,128)(2,1)} %collective-permute-done), channel_id=1, source_target_pairs={{0,8},{4,12},{8,16},{12,20},{16,24},{20,28},{24,32},{28,36},{32,40... | collective-permute-start | bytes 1191944 | tf_op jit(solution)/shard_map/ppermute | solution.py:274
  37.2 8.7 %all-to-all-done.lefts = bf16[4,1552,128]{2,1,0:T(8,128)(2,1)S(1)} async-done(((bf16[4,1552,128]{2,1,0:T(8,128)(2,1)}), bf16[4,1552,128]{2,1,0:T(8,128)(2,1)S(1)}, u32[]{:S(2)}, u32[]{:S(2)}) %all-to-all-start) | async-done | bytes 1589280 | tf_op jit(solution)/shard_map/all_to_all | solution.py:260
  45.8 0.1 spread.1
  46.0 26.3 %all_to_all.10.tab_ref = s32[128,1,128]{2,1,0:T(1,128)S(1)} all-to-all(s32[128,1,128]{2,1,0:T(1,128)S(1)} %spread.1), channel_id=1, replica_groups=mesh['rows_0'=16,'rows_1'=4,'rows_2'=2,'cols'=4] {'rows_0','rows_1','row..., dimensions={0} | all-to-all | bytes 131072 | tf_op jit(solution)/shard_map/all_to_all | solution.py:260
  72.3 0.9 %starts.1 = s32[1,4]{1,0:T(1,128)} custom-call(s32[128,1,128]{2,1,0:T(1,128)S(1)} %all_to_all.10.tab_ref), custom_call_target="tpu_custom_call" | custom-call | tf_op jit(solution)/shard_map/starts/pallas_call | solution.py:222
  73.2 0.0 collective-permute-done.4.far_ref
  73.2 0.0 collective-permute-done.3.back_ref
  73.2 0.0 collective-permute-done.2.swap_ref
  73.2 8.2 %square.1 = (bf16[4,36,128,128]{3,2,1,0:T(8,128)(2,1)}, s32[4,36]{1,0:T(4,128)}) custom-call(bf16[4,1552,128]{2,1,0:T(8,128)(2,1)S(1)} %all-to-all-done.lefts, bf16[3,1552,128]{2,1,0:T(8,128)(2,1)S(1)} %pad_maximum_fusion.trio_ref, bf16[3,1552,128]{2,1,0:T(8,128)(2,1)} %collective-permute-done.2.swap_ref, bf16[1552,128]{1,0:T(8,128)(2,1)} %collective-permute-done.3.back_ref, ...), custom_call_target="tpu_custom_call" | custom-call | tf_op jit(solution)/shard_map/square/pallas_call | solution.py:234
  (1 shorter events, 0.0 us)
Async XLA Ops:
  3.4 23.6 %collective-permute-start = (bf16[1552,128]{1,0:T(8,128)(2,1)}, bf16[1552,128]{1,0:T(8,128)(2,1)}, u32[]{:S(2)}, u32[]{:S(2)}) collective-permute-start(bf16[1552,128]{1,0:T(8,128)(2,1)} %get-tuple-element.11), channel_id=1, source_target_pairs={{0,8},{4,12},{8,16},{12,20},{16,24},{20,28},{24,32},{28,36},{32,40... | collective-permute-start | bytes 1191944 | tf_op jit(solution)/shard_map/ppermute | solution.py:274
  7.4 20.5 %collective-permute-start.1 = (bf16[1552,128]{1,0:T(8,128)(2,1)}, bf16[1552,128]{1,0:T(8,128)(2,1)S(1)}, u32[]{:S(2)}, u32[]{:S(2)}) collective-permute-start(bf16[1552,128]{1,0:T(8,128)(2,1)} %get-tuple-element.11), channel_id=1, source_target_pairs={{0,504},{4,508},{8,0},{12,4},{16,8},{20,12},{24,16},{28,20},{32,24... | collective-permute-start | bytes 1191944 | tf_op jit(solution)/shard_map/ppermute | solution.py:274
  22.1 23.8 %all-to-all-start = ((bf16[4,1552,128]{2,1,0:T(8,128)(2,1)}), bf16[4,1552,128]{2,1,0:T(8,128)(2,1)S(1)}, u32[]{:S(2)}, u32[]{:S(2)}) async-start(bf16[4,1552,128]{2,1,0:T(8,128)(2,1)} %broadcast_in_dim.14), calls=%async_computation | async-start | bytes 3178496 | tf_op jit(solution)/shard_map/all_to_all | solution.py:260
  27.9 0.7 copy-start
  29.9 43.4 %collective-permute-start.2 = (bf16[3,1552,128]{2,1,0:T(8,128)(2,1)S(1)}, bf16[3,1552,128]{2,1,0:T(8,128)(2,1)}, u32[]{:S(2)}, u32[]{:S(2)}) collective-permute-start(bf16[3,1552,128]{2,1,0:T(8,128)(2,1)S(1)} %pad_maximum_fusion.trio_ref), channel_id=1, source_target_pairs={{0,4},{4,0},{1,5},{5,1},{2,6},{6,2},{3,7},{7,3},{8,12},{12,8},{9,1... | collective-permute-start | bytes 3575816 | tf_op jit(solution)/shard_map/ppermute | solution.py:264
  33.3 39.9 %collective-permute-start.4 = (bf16[1552,128]{1,0:T(8,128)(2,1)}, bf16[1552,128]{1,0:T(8,128)(2,1)S(1)}, u32[]{:S(2)}, u32[]{:S(2)}) collective-permute-start(bf16[1552,128]{1,0:T(8,128)(2,1)} %get-tuple-element.11), channel_id=1, source_target_pairs={{0,500},{4,16},{8,508},{12,24},{16,4},{20,32},{24,12},{28,40},{32,... | collective-permute-start | bytes 1191944 | tf_op jit(solution)/shard_map/ppermute | solution.py:274
  35.2 38.0 %collective-permute-start.3 = (bf16[1552,128]{1,0:T(8,128)(2,1)}, bf16[1552,128]{1,0:T(8,128)(2,1)}, u32[]{:S(2)}, u32[]{:S(2)}) collective-permute-start(bf16[1552,128]{1,0:T(8,128)(2,1)} %collective-permute-done), channel_id=1, source_target_pairs={{0,8},{4,12},{8,16},{12,20},{16,24},{20,28},{24,32},{28,36},{32,40... | collective-permute-start | bytes 1191944 | tf_op jit(solution)/shard_map/ppermute | solution.py:274

commit v2 on v0

--- a/solution.py
+++ b/solution.py
@@ -27,7 +27,10 @@
     return lax.axis_index(ROWS), lax.axis_index("cols")
 
 
-def spread_kernel(cols_ref, out_ref):
+def spread_kernel(held_ref, out_ref, cols_ref, sem):
+    copy = pltpu.make_async_copy(held_ref, cols_ref, sem)
+    copy.start()
+    copy.wait()
     lane = lax.broadcasted_iota(jnp.int32, (1, BS), 1)
     row = jnp.zeros((1, BS), jnp.int32)
     for r in range(PB):
@@ -195,11 +198,12 @@
     return pl.pallas_call(
         spread_kernel,
         out_shape=jax.ShapeDtypeStruct((FAR, 1, BS), jnp.int32),
-        in_specs=[SMEM],
+        in_specs=[HBM],
         out_specs=VMEM,
+        scratch_shapes=[pltpu.SMEM((KG, 1, PB), jnp.int32), pltpu.SemaphoreType.DMA],
         compiler_params=pltpu.CompilerParams(vmem_limit_bytes=8 << 20),
         name="spread",
-    )(cols)
+    )(pltpu.with_memory_space_constraint(cols, pltpu.HBM))
 
 
 def turned_table(parts):

time: 92.9 us -> 93 us (level)
  no operation moved by 1% of the time
where the time goes in v2:
time: 93 us; the launch traced here: 92.6 us
  starting transfers between devices  34.4 us (37%)
  blocking collectives  30.2 us (32%)
  waiting for transfers between devices  18.5 us (20%)
  Pallas kernels  7.57 us (8%)
  other arithmetic  1.2 us (1%)
    all_to_all x2, blocking collectives, exchange(): return lax.all_to_all(array, axes, 0, 0, tiled=True)  30.2 us
    ppermute x4, starting transfers between devices, sent_on(): return lax.ppermute(block, ROWS, route)  20.1 us
    ppermute x4, waiting for transfers between devices, sent_on(): return lax.ppermute(block, ROWS, route)  18.5 us
    ppermute x3, starting transfers between devices, turned(): lax.ppermute(block, 'cols', [((c + distance) % GROUPS, c) for c in range(...  10.5 us
    pallas_call x1, Pallas kernels, square(): pl.pallas_call(square_kernel, out_shape=jax.ShapeDtypeStruct((PB, WIDTH,...  5.7 us
    ppermute x1, starting transfers between devices, swapped(): return lax.ppermute(block, 'rows_2', [(0, 1), (1, 0)])  3.72 us
  transfers between devices with their start and end apart: 8, of which 3 were waited for; matrix products, arithmetic and copies ran while one was open for 0% of the time, Pallas kernels for 2%

profile of v2, /device:TPU:1, one launch (start us, length us, event | category | flops | bytes accessed | tf_op | source)
XLA Modules:
  0.0 92.6 jit_solution(8412225777733411584)
XLA Ops:
  0.6 14.4 %collective-permute-start.4 = (bf16[4,3,128,128]{3,2,1,0:T(8,128)(2,1)}, bf16[4,3,128,128]{3,2,1,0:T(8,128)(2,1)S(1)}, u32[]{:S(2)}, u32[]{:S(2)}) collective-permute-start(bf16[4,3,128,128]{3,2,1,0:T(8,128)(2,1)} %bitcast.13), channel_id=1, source_target_pairs={{0,504},{4,508},{8,0},{12,4},{16,8},{20,12},{24,16},{28,20},{32,24... | collective-permute-start | bytes 1179656 | tf_op jit(solution)/shard_map/ppermute | solution.py:276
  15.0 1.9 %collective-permute-start.3 = (bf16[4,3,128,128]{3,2,1,0:T(8,128)(2,1)}, bf16[4,3,128,128]{3,2,1,0:T(8,128)(2,1)S(1)}, u32[]{:S(2)}, u32[]{:S(2)}) collective-permute-start(bf16[4,3,128,128]{3,2,1,0:T(8,128)(2,1)} %bitcast.14), channel_id=1, source_target_pairs={{0,8},{4,12},{8,16},{12,20},{16,24},{20,28},{24,32},{28,36},{32,40... | collective-permute-start | bytes 1179656 | tf_op jit(solution)/shard_map/ppermute | solution.py:276
  17.0 6.2 %collective-permute-done.4 = bf16[4,3,128,128]{3,2,1,0:T(8,128)(2,1)S(1)} collective-permute-done((bf16[4,3,128,128]{3,2,1,0:T(8,128)(2,1)}, bf16[4,3,128,128]{3,2,1,0:T(8,128)(2,1)S(1)}, u32[]{:S(2)}, u32[]{:S(2)}) %collective-permute-start.4) | collective-permute-done | bytes 393248 | tf_op jit(solution)/shard_map/ppermute | solution.py:276
  23.1 7.1 %collective-permute-done.3 = bf16[4,3,128,128]{3,2,1,0:T(8,128)(2,1)S(1)} collective-permute-done((bf16[4,3,128,128]{3,2,1,0:T(8,128)(2,1)}, bf16[4,3,128,128]{3,2,1,0:T(8,128)(2,1)S(1)}, u32[]{:S(2)}, u32[]{:S(2)}) %collective-permute-start.3) | collective-permute-done | bytes 393248 | tf_op jit(solution)/shard_map/ppermute | solution.py:276
  30.2 0.0 copy-start
  30.2 1.2 %pad_maximum_fusion.trio_ref = bf16[3,4,3,128,128]{4,3,2,1,0:T(8,128)(2,1)S(1)} fusion(bf16[1,4,3,128,128]{4,3,2,1,0:T(8,128)(2,1)S(1)} %bitcast.21, bf16[1,4,3,128,128]{4,3,2,1,0:T(8,128)(2,1)S(1)} %bitcast.20, bf16[1,4,3,128,128]{4,3,2,1,0:T(8,128)(2,1)} %bitcast.15), kind=kLoop, calls=%fused_computation | loop fusion | flops 1179648 | bytes 2359296 | tf_op jit(solution)/shard_map/stack | solution.py:291
  31.4 3.7 %collective-permute-start.5 = (bf16[3,4,3,128,128]{4,3,2,1,0:T(8,128)(2,1)S(1)}, bf16[3,4,3,128,128]{4,3,2,1,0:T(8,128)(2,1)S(1)}, u32[]{:S(2)}, u32[]{:S(2)}) collective-permute-start(bf16[3,4,3,128,128]{4,3,2,1,0:T(8,128)(2,1)S(1)} %pad_maximum_fusion.trio_ref), channel_id=1, source_target_pairs={{0,4},{4,0},{1,5},{5,1},{2,6},{6,2},{3,7},{7,3},{8,12},{12,8},{9,1... | collective-permute-start | bytes 3538952 | tf_op jit(solution)/shard_map/ppermute | solution.py:262
  35.1 0.0 copy-done
  35.1 1.9 %collective-permute-start.7 = (bf16[4,3,128,128]{3,2,1,0:T(8,128)(2,1)S(1)}, bf16[4,3,128,128]{3,2,1,0:T(8,128)(2,1)S(1)}, u32[]{:S(2)}, u32[]{:S(2)}) collective-permute-start(bf16[4,3,128,128]{3,2,1,0:T(8,128)(2,1)S(1)} %bitcast.16), channel_id=1, source_target_pairs={{0,500},{4,16},{8,508},{12,24},{16,4},{20,32},{24,12},{28,40},{32,... | collective-permute-start | bytes 1179656 | tf_op jit(solution)/shard_map/ppermute | solution.py:276
  37.0 3.1 %collective-permute-start.2 = (bf16[4,3,128,128]{3,2,1,0:T(8,128)(2,1)S(1)}, bf16[4,3,128,128]{3,2,1,0:T(8,128)(2,1)S(1)}, u32[]{:S(2)}, u32[]{:S(2)}) collective-permute-start(bf16[4,3,128,128]{3,2,1,0:T(8,128)(2,1)S(1)} %bitcast.17), channel_id=1, source_target_pairs={{3,0},{0,1},{1,2},{2,3},{7,4},{4,5},{5,6},{6,7},{11,8},{8,9},{9,10... | collective-permute-start | bytes 1179656 | tf_op jit(solution)/shard_map/ppermute | solution.py:266
  40.2 4.4 %collective-permute-start.1 = (bf16[4,3,128,128]{3,2,1,0:T(8,128)(2,1)S(1)}, bf16[4,3,128,128]{3,2,1,0:T(8,128)(2,1)S(1)}, u32[]{:S(2)}, u32[]{:S(2)}) collective-permute-start(bf16[4,3,128,128]{3,2,1,0:T(8,128)(2,1)S(1)} %bitcast.18), channel_id=1, source_target_pairs={{2,0},{3,1},{0,2},{1,3},{6,4},{7,5},{4,6},{5,7},{10,8},{11,9},{8,1... | collective-permute-start | bytes 1179656 | tf_op jit(solution)/shard_map/ppermute | solution.py:266
  44.5 3.1 %collective-permute-start = (bf16[4,3,128,128]{3,2,1,0:T(8,128)(2,1)S(1)}, bf16[4,3,128,128]{3,2,1,0:T(8,128)(2,1)S(1)}, u32[]{:S(2)}, u32[]{:S(2)}) collective-permute-start(bf16[4,3,128,128]{3,2,1,0:T(8,128)(2,1)S(1)} %bitcast.19), channel_id=1, source_target_pairs={{1,0},{2,1},{3,2},{0,3},{5,4},{6,5},{7,6},{4,7},{9,8},{10,9},{11,1... | collective-permute-start | bytes 1179656 | tf_op jit(solution)/shard_map/ppermute | solution.py:266
  47.6 5.3 %collective-permute-done.7.far_ref = bf16[4,3,128,128]{3,2,1,0:T(8,128)(2,1)S(1)} collective-permute-done((bf16[4,3,128,128]{3,2,1,0:T(8,128)(2,1)S(1)}, bf16[4,3,128,128]{3,2,1,0:T(8,128)(2,1)S(1)}, u32[]{:S(2)}, u32[]{:S(2)}) %collective-permute-start.7) | collective-permute-done | bytes 393248 | tf_op jit(solution)/shard_map/ppermute | solution.py:276
  52.9 1.9 %collective-permute-start.6 = (bf16[4,3,128,128]{3,2,1,0:T(8,128)(2,1)S(1)}, bf16[4,3,128,128]{3,2,1,0:T(8,128)(2,1)S(1)}, u32[]{:S(2)}, u32[]{:S(2)}) collective-permute-start(bf16[4,3,128,128]{3,2,1,0:T(8,128)(2,1)S(1)} %collective-permute-done.3), channel_id=1, source_target_pairs={{0,8},{4,12},{8,16},{12,20},{16,24},{20,28},{24,32},{28,36},{32,40... | collective-permute-start | bytes 1179656 | tf_op jit(solution)/shard_map/ppermute | solution.py:276
  54.8 0.7 spread.1
  55.5 14.6 %all_to_all.10.in_ref = s32[32,1,128]{2,1,0:T(1,128)S(1)} all-to-all(s32[32,1,128]{2,1,0:T(1,128)S(1)} %spread.1), channel_id=1, replica_groups=mesh['rows_0'=16,'rows_1'=4,'rows_2'=2,'cols'=4] {'rows_0','rows_2'}, dimensions={0} | all-to-all | bytes 32768 | tf_op jit(solution)/shard_map/all_to_all | solution.py:258
  70.2 0.1 turned_table.1
  70.2 15.5 %all_to_all.11.tab_ref = s32[16,16,128]{2,1,0:T(8,128)S(1)} all-to-all(s32[16,16,128]{2,1,0:T(8,128)S(1)} %turned_table.1), channel_id=1, replica_groups=mesh['rows_0'=16,'rows_1'=4,'rows_2'=2,'cols'=4] {'rows_1','cols'}, dimensions={0} | all-to-all | bytes 262144 | tf_op jit(solution)/shard_map/all_to_all | solution.py:258
  85.8 1.1 %indices.1 = (s32[4,36]{1,0:T(4,128)}, s32[1,4]{1,0:T(1,128)}, s32[16,128]{1,0:T(8,128)S(1)}) custom-call(s32[16,16,128]{2,1,0:T(8,128)S(1)} %all_to_all.11.tab_ref), custom_call_target="tpu_custom_call" | custom-call | tf_op jit(solution)/shard_map/indices/pallas_call | solution.py:222
  86.9 0.0 collective-permute-done.2.down_ref
  86.9 0.0 collective-permute-done.1.over_ref
  86.9 0.0 collective-permute-done.up_ref
  86.9 0.0 collective-permute-done.6.back_ref
  86.9 0.0 collective-permute-done.5.swap_ref
  86.9 5.7 %square.1 = bf16[4,36,128,128]{3,2,1,0:T(8,128)(2,1)} custom-call(s32[16,128]{1,0:T(8,128)S(1)} %get-tuple-element.6.map_ref, bf16[4,3,128,128]{3,2,1,0:T(8,128)(2,1)S(1)} %collective-permute-done.up_ref, bf16[4,3,128,128]{3,2,1,0:T(8,128)(2,1)S(1)} %collective-permute-done.1.over_ref, bf16[4,3,128,128]{3,2,1,0:T(8,128)(2,1)S(1)} %collective-permute-done.2.down_ref, ...), custom_call_target="tpu_custom_call" | custom-call | tf_op jit(solution)/shard_map/square/pallas_call | solution.py:238
Async XLA Ops:
  0.6 22.5 %collective-permute-start.4 = (bf16[4,3,128,128]{3,2,1,0:T(8,128)(2,1)}, bf16[4,3,128,128]{3,2,1,0:T(8,128)(2,1)S(1)}, u32[]{:S(2)}, u32[]{:S(2)}) collective-permute-start(bf16[4,3,128,128]{3,2,1,0:T(8,128)(2,1)} %bitcast.13), channel_id=1, source_target_pairs={{0,504},{4,508},{8,0},{12,4},{16,8},{20,12},{24,16},{28,20},{32,24... | collective-permute-start | bytes 1179656 | tf_op jit(solution)/shard_map/ppermute | solution.py:276
  15.0 15.1 %collective-permute-start.3 = (bf16[4,3,128,128]{3,2,1,0:T(8,128)(2,1)}, bf16[4,3,128,128]{3,2,1,0:T(8,128)(2,1)S(1)}, u32[]{:S(2)}, u32[]{:S(2)}) collective-permute-start(bf16[4,3,128,128]{3,2,1,0:T(8,128)(2,1)} %bitcast.14), channel_id=1, source_target_pairs={{0,8},{4,12},{8,16},{12,20},{16,24},{20,28},{24,32},{28,36},{32,40... | collective-permute-start | bytes 1179656 | tf_op jit(solution)/shard_map/ppermute | solution.py:276
  30.2 4.9 %copy-start = (bf16[4,1,3,128,128]{4,3,2,1,0:T(8,128)(2,1)S(1)}, bf16[4,1,3,128,128]{4,3,2,1,0:T(8,128)(2,1)}, u32[]{:S(2)}) copy-start(bf16[4,1,3,128,128]{4,3,2,1,0:T(8,128)(2,1)} %param.2) | copy-start | bytes 1179652
  31.4 55.5 %collective-permute-start.5 = (bf16[3,4,3,128,128]{4,3,2,1,0:T(8,128)(2,1)S(1)}, bf16[3,4,3,128,128]{4,3,2,1,0:T(8,128)(2,1)S(1)}, u32[]{:S(2)}, u32[]{:S(2)}) collective-permute-start(bf16[3,4,3,128,128]{4,3,2,1,0:T(8,128)(2,1)S(1)} %pad_maximum_fusion.trio_ref), channel_id=1, source_target_pairs={{0,4},{4,0},{1,5},{5,1},{2,6},{6,2},{3,7},{7,3},{8,12},{12,8},{9,1... | collective-permute-start | bytes 3538952 | tf_op jit(solution)/shard_map/ppermute | solution.py:262
  35.1 17.8 %collective-permute-start.7 = (bf16[4,3,128,128]{3,2,1,0:T(8,128)(2,1)S(1)}, bf16[4,3,128,128]{3,2,1,0:T(8,128)(2,1)S(1)}, u32[]{:S(2)}, u32[]{:S(2)}) collective-permute-start(bf16[4,3,128,128]{3,2,1,0:T(8,128)(2,1)S(1)} %bitcast.16), channel_id=1, source_target_pairs={{0,500},{4,16},{8,508},{12,24},{16,4},{20,32},{24,12},{28,40},{32,... | collective-permute-start | bytes 1179656 | tf_op jit(solution)/shard_map/ppermute | solution.py:276
  37.0 49.8 %collective-permute-start.2 = (bf16[4,3,128,128]{3,2,1,0:T(8,128)(2,1)S(1)}, bf16[4,3,128,128]{3,2,1,0:T(8,128)(2,1)S(1)}, u32[]{:S(2)}, u32[]{:S(2)}) collective-permute-start(bf16[4,3,128,128]{3,2,1,0:T(8,128)(2,1)S(1)} %bitcast.17), channel_id=1, source_target_pairs={{3,0},{0,1},{1,2},{2,3},{7,4},{4,5},{5,6},{6,7},{11,8},{8,9},{9,10... | collective-permute-start | bytes 1179656 | tf_op jit(solution)/shard_map/ppermute | solution.py:266
  40.2 46.7 %collective-permute-start.1 = (bf16[4,3,128,128]{3,2,1,0:T(8,128)(2,1)S(1)}, bf16[4,3,128,128]{3,2,1,0:T(8,128)(2,1)S(1)}, u32[]{:S(2)}, u32[]{:S(2)}) collective-permute-start(bf16[4,3,128,128]{3,2,1,0:T(8,128)(2,1)S(1)} %bitcast.18), channel_id=1, source_target_pairs={{2,0},{3,1},{0,2},{1,3},{6,4},{7,5},{4,6},{5,7},{10,8},{11,9},{8,1... | collective-permute-start | bytes 1179656 | tf_op jit(solution)/shard_map/ppermute | solution.py:266
  44.5 42.3 %collective-permute-start = (bf16[4,3,128,128]{3,2,1,0:T(8,128)(2,1)S(1)}, bf16[4,3,128,128]{3,2,1,0:T(8,128)(2,1)S(1)}, u32[]{:S(2)}, u32[]{:S(2)}) collective-permute-start(bf16[4,3,128,128]{3,2,1,0:T(8,128)(2,1)S(1)} %bitcast.19), channel_id=1, source_target_pairs={{1,0},{2,1},{3,2},{0,3},{5,4},{6,5},{7,6},{4,7},{9,8},{10,9},{11,1... | collective-permute-start | bytes 1179656 | tf_op jit(solution)/shard_map/ppermute | solution.py:266
  52.9 34.0 %collective-permute-start.6 = (bf16[4,3,128,128]{3,2,1,0:T(8,128)(2,1)S(1)}, bf16[4,3,128,128]{3,2,1,0:T(8,128)(2,1)S(1)}, u32[]{:S(2)}, u32[]{:S(2)}) collective-permute-start(bf16[4,3,128,128]{3,2,1,0:T(8,128)(2,1)S(1)} %collective-permute-done.3), channel_id=1, source_target_pairs={{0,8},{4,12},{8,16},{12,20},{16,24},{20,28},{24,32},{28,36},{32,40... | collective-permute-start | bytes 1179656 | tf_op jit(solution)/shard_map/ppermute | solution.py:276

commit v3 on v2

--- a/solution.py
+++ b/solution.py
@@ -17,10 +17,10 @@
 WIN = 2 * HP
 ROWS = ("rows_0", "rows_1", "rows_2")
 ROOM = 16
-FAR = 32
-NEAR = 16
-FAR_AXES = ("rows_0", "rows_2")
-NEAR_AXES = ("rows_1", "cols")
+FAR = 64
+NEAR = 8
+FAR_AXES = ("rows_0", "rows_1")
+NEAR_AXES = ("rows_2", "cols")
 
 
 def place():
@@ -43,10 +43,10 @@
     p0, _ = place()
     table_ref[...] = jnp.zeros((NP, BS), jnp.int32)
     for n in range(FAR):
-        spot = 8 * (n // 2) + (p0 & 6) + n % 2
+        spot = 2 * n + (p0 & 1)
         table_ref[pl.ds(spot, 1), :] = in_ref[n]
-    turned = jnp.transpose(table_ref[...])
-    out_ref[...] = jnp.broadcast_to(turned[None, :ROOM], out_ref.shape)
+    turned = jnp.transpose(table_ref[...])[:ROOM].astype(jnp.float32).astype(jnp.bfloat16)
+    out_ref[...] = jnp.broadcast_to(turned[None], out_ref.shape)
 
 
 def bits_set(x):
@@ -59,8 +59,8 @@
 def index_kernel(tab_ref, cols_ref, starts_ref, map_ref, turned_ref):
     p0, c = place()
     spot = lax.broadcasted_iota(jnp.int32, (GROUPS * ROOM, NP), 1)
-    parts = [tab_ref[GROUPS * n : GROUPS * (n + 1)] for n in range(NEAR // GROUPS)]
-    turned = ((parts[0] + parts[1]) + (parts[2] + parts[3])).reshape(GROUPS * ROOM, NP)
+    parts = [tab_ref[GROUPS * n : GROUPS * (n + 1)].astype(jnp.float32) for n in range(2)]
+    turned = (parts[0] + parts[1]).astype(jnp.int32).reshape(GROUPS * ROOM, NP)
     turned = (turned - spot + HP) & (NP - 1)
     turned_ref[...] = turned
     panel = lax.broadcasted_iota(jnp.int32, (1, NP), 1)
@@ -209,7 +209,7 @@
 def turned_table(parts):
     return pl.pallas_call(
         turn_kernel,
-        out_shape=jax.ShapeDtypeStruct((NEAR, ROOM, BS), jnp.int32),
+        out_shape=jax.ShapeDtypeStruct((NEAR, ROOM, BS), jnp.bfloat16),
         in_specs=[VMEM],
         out_specs=VMEM,
         scratch_shapes=[pltpu.VMEM((NP, BS), jnp.int32)],
@@ -231,7 +231,7 @@
         scratch_shapes=[pltpu.VMEM((GROUPS * ROOM, NP), jnp.int32)],
         compiler_params=pltpu.CompilerParams(vmem_limit_bytes=8 << 20),
         name="indices",
-    )(table)
+    )(near_core(table))
 
 
 def square(where, lefts, pieces):

time: 93 us -> 93.6 us (level)
  no operation moved by 1% of the time
where the time goes in v3:
time: 93.6 us; the launch traced here: 93.2 us
  starting transfers between devices  34.4 us (37%)
  blocking collectives  30.7 us (33%)
  waiting for transfers between devices  18.5 us (20%)
  Pallas kernels  7.6 us (8%)
  other arithmetic  1.2 us (1%)
    all_to_all x2, blocking collectives, exchange(): return lax.all_to_all(array, axes, 0, 0, tiled=True)  30.7 us
    ppermute x4, starting transfers between devices, sent_on(): return lax.ppermute(block, ROWS, route)  20.1 us
    ppermute x4, waiting for transfers between devices, sent_on(): return lax.ppermute(block, ROWS, route)  18.5 us
    ppermute x3, starting transfers between devices, turned(): lax.ppermute(block, 'cols', [((c + distance) % GROUPS, c) for c in range(...  10.5 us
    pallas_call x1, Pallas kernels, square(): pl.pallas_call(square_kernel, out_shape=jax.ShapeDtypeStruct((PB, WIDTH,...  5.7 us
    ppermute x1, starting transfers between devices, swapped(): return lax.ppermute(block, 'rows_2', [(0, 1), (1, 0)])  3.72 us
  transfers between devices with their start and end apart: 8, of which 3 were waited for; matrix products, arithmetic and copies ran while one was open for 0% of the time, Pallas kernels for 2%

profile of v3, /device:TPU:1, one launch (start us, length us, event | category | flops | bytes accessed | tf_op | source)
XLA Modules:
  0.0 93.2 jit_solution(14943157635399156498)
XLA Ops:
  0.6 14.4 %collective-permute-start.4 = (bf16[4,3,128,128]{3,2,1,0:T(8,128)(2,1)}, bf16[4,3,128,128]{3,2,1,0:T(8,128)(2,1)S(1)}, u32[]{:S(2)}, u32[]{:S(2)}) collective-permute-start(bf16[4,3,128,128]{3,2,1,0:T(8,128)(2,1)} %bitcast.13), channel_id=1, source_target_pairs={{0,504},{4,508},{8,0},{12,4},{16,8},{20,12},{24,16},{28,20},{32,24... | collective-permute-start | bytes 1179656 | tf_op jit(solution)/shard_map/ppermute | solution.py:276
  15.0 1.9 %collective-permute-start.3 = (bf16[4,3,128,128]{3,2,1,0:T(8,128)(2,1)}, bf16[4,3,128,128]{3,2,1,0:T(8,128)(2,1)S(1)}, u32[]{:S(2)}, u32[]{:S(2)}) collective-permute-start(bf16[4,3,128,128]{3,2,1,0:T(8,128)(2,1)} %bitcast.14), channel_id=1, source_target_pairs={{0,8},{4,12},{8,16},{12,20},{16,24},{20,28},{24,32},{28,36},{32,40... | collective-permute-start | bytes 1179656 | tf_op jit(solution)/shard_map/ppermute | solution.py:276
  17.0 6.2 %collective-permute-done.4 = bf16[4,3,128,128]{3,2,1,0:T(8,128)(2,1)S(1)} collective-permute-done((bf16[4,3,128,128]{3,2,1,0:T(8,128)(2,1)}, bf16[4,3,128,128]{3,2,1,0:T(8,128)(2,1)S(1)}, u32[]{:S(2)}, u32[]{:S(2)}) %collective-permute-start.4) | collective-permute-done | bytes 393248 | tf_op jit(solution)/shard_map/ppermute | solution.py:276
  23.1 7.1 %collective-permute-done.3 = bf16[4,3,128,128]{3,2,1,0:T(8,128)(2,1)S(1)} collective-permute-done((bf16[4,3,128,128]{3,2,1,0:T(8,128)(2,1)}, bf16[4,3,128,128]{3,2,1,0:T(8,128)(2,1)S(1)}, u32[]{:S(2)}, u32[]{:S(2)}) %collective-permute-start.3) | collective-permute-done | bytes 393248 | tf_op jit(solution)/shard_map/ppermute | solution.py:276
  30.2 0.0 copy-start
  30.2 1.2 %pad_maximum_fusion.trio_ref = bf16[3,4,3,128,128]{4,3,2,1,0:T(8,128)(2,1)S(1)} fusion(bf16[1,4,3,128,128]{4,3,2,1,0:T(8,128)(2,1)S(1)} %bitcast.21, bf16[1,4,3,128,128]{4,3,2,1,0:T(8,128)(2,1)S(1)} %bitcast.20, bf16[1,4,3,128,128]{4,3,2,1,0:T(8,128)(2,1)} %bitcast.15), kind=kLoop, calls=%fused_computation | loop fusion | flops 1179648 | bytes 2359296 | tf_op jit(solution)/shard_map/stack | solution.py:291
  31.4 3.7 %collective-permute-start.5 = (bf16[3,4,3,128,128]{4,3,2,1,0:T(8,128)(2,1)S(1)}, bf16[3,4,3,128,128]{4,3,2,1,0:T(8,128)(2,1)S(1)}, u32[]{:S(2)}, u32[]{:S(2)}) collective-permute-start(bf16[3,4,3,128,128]{4,3,2,1,0:T(8,128)(2,1)S(1)} %pad_maximum_fusion.trio_ref), channel_id=1, source_target_pairs={{0,4},{4,0},{1,5},{5,1},{2,6},{6,2},{3,7},{7,3},{8,12},{12,8},{9,1... | collective-permute-start | bytes 3538952 | tf_op jit(solution)/shard_map/ppermute | solution.py:262
  35.1 0.0 copy-done
  35.1 1.9 %collective-permute-start.7 = (bf16[4,3,128,128]{3,2,1,0:T(8,128)(2,1)S(1)}, bf16[4,3,128,128]{3,2,1,0:T(8,128)(2,1)S(1)}, u32[]{:S(2)}, u32[]{:S(2)}) collective-permute-start(bf16[4,3,128,128]{3,2,1,0:T(8,128)(2,1)S(1)} %bitcast.16), channel_id=1, source_target_pairs={{0,500},{4,16},{8,508},{12,24},{16,4},{20,32},{24,12},{28,40},{32,... | collective-permute-start | bytes 1179656 | tf_op jit(solution)/shard_map/ppermute | solution.py:276
  37.0 3.1 %collective-permute-start.2 = (bf16[4,3,128,128]{3,2,1,0:T(8,128)(2,1)S(1)}, bf16[4,3,128,128]{3,2,1,0:T(8,128)(2,1)S(1)}, u32[]{:S(2)}, u32[]{:S(2)}) collective-permute-start(bf16[4,3,128,128]{3,2,1,0:T(8,128)(2,1)S(1)} %bitcast.17), channel_id=1, source_target_pairs={{3,0},{0,1},{1,2},{2,3},{7,4},{4,5},{5,6},{6,7},{11,8},{8,9},{9,10... | collective-permute-start | bytes 1179656 | tf_op jit(solution)/shard_map/ppermute | solution.py:266
  40.2 4.4 %collective-permute-start.1 = (bf16[4,3,128,128]{3,2,1,0:T(8,128)(2,1)S(1)}, bf16[4,3,128,128]{3,2,1,0:T(8,128)(2,1)S(1)}, u32[]{:S(2)}, u32[]{:S(2)}) collective-permute-start(bf16[4,3,128,128]{3,2,1,0:T(8,128)(2,1)S(1)} %bitcast.18), channel_id=1, source_target_pairs={{2,0},{3,1},{0,2},{1,3},{6,4},{7,5},{4,6},{5,7},{10,8},{11,9},{8,1... | collective-permute-start | bytes 1179656 | tf_op jit(solution)/shard_map/ppermute | solution.py:266
  44.5 3.1 %collective-permute-start = (bf16[4,3,128,128]{3,2,1,0:T(8,128)(2,1)S(1)}, bf16[4,3,128,128]{3,2,1,0:T(8,128)(2,1)S(1)}, u32[]{:S(2)}, u32[]{:S(2)}) collective-permute-start(bf16[4,3,128,128]{3,2,1,0:T(8,128)(2,1)S(1)} %bitcast.19), channel_id=1, source_target_pairs={{1,0},{2,1},{3,2},{0,3},{5,4},{6,5},{7,6},{4,7},{9,8},{10,9},{11,1... | collective-permute-start | bytes 1179656 | tf_op jit(solution)/shard_map/ppermute | solution.py:266
  47.6 5.3 %collective-permute-done.7.far_ref = bf16[4,3,128,128]{3,2,1,0:T(8,128)(2,1)S(1)} collective-permute-done((bf16[4,3,128,128]{3,2,1,0:T(8,128)(2,1)S(1)}, bf16[4,3,128,128]{3,2,1,0:T(8,128)(2,1)S(1)}, u32[]{:S(2)}, u32[]{:S(2)}) %collective-permute-start.7) | collective-permute-done | bytes 393248 | tf_op jit(solution)/shard_map/ppermute | solution.py:276
  52.9 1.9 %collective-permute-start.6 = (bf16[4,3,128,128]{3,2,1,0:T(8,128)(2,1)S(1)}, bf16[4,3,128,128]{3,2,1,0:T(8,128)(2,1)S(1)}, u32[]{:S(2)}, u32[]{:S(2)}) collective-permute-start(bf16[4,3,128,128]{3,2,1,0:T(8,128)(2,1)S(1)} %collective-permute-done.3), channel_id=1, source_target_pairs={{0,8},{4,12},{8,16},{12,20},{16,24},{20,28},{24,32},{28,36},{32,40... | collective-permute-start | bytes 1179656 | tf_op jit(solution)/shard_map/ppermute | solution.py:276
  54.8 0.7 spread.1
  55.5 20.6 %all_to_all.10.in_ref = s32[64,1,128]{2,1,0:T(1,128)S(1)} all-to-all(s32[64,1,128]{2,1,0:T(1,128)S(1)} %spread.1), channel_id=1, replica_groups=mesh['rows_0'=16,'rows_1'=4,'rows_2'=2,'cols'=4] {'rows_0','rows_1'}, dimensions={0} | all-to-all | bytes 65536 | tf_op jit(solution)/shard_map/all_to_all | solution.py:258
  76.1 0.1 turned_table.1
  76.2 10.1 %all_to_all.11.tab_ref = bf16[8,16,128]{2,1,0:T(8,128)(2,1)S(1)} all-to-all(bf16[8,16,128]{2,1,0:T(8,128)(2,1)S(1)} %turned_table.1), channel_id=1, replica_groups=mesh['rows_0'=16,'rows_1'=4,'rows_2'=2,'cols'=4] {'rows_2','cols'}, dimensions={0} | all-to-all | bytes 65536 | tf_op jit(solution)/shard_map/all_to_all | solution.py:258
  86.3 1.1 %indices.1 = (s32[4,36]{1,0:T(4,128)}, s32[1,4]{1,0:T(1,128)}, s32[16,128]{1,0:T(8,128)S(1)}) custom-call(bf16[8,16,128]{2,1,0:T(8,128)(2,1)S(1)} %all_to_all.11.tab_ref), custom_call_target="tpu_custom_call" | custom-call | tf_op jit(solution)/shard_map/indices/pallas_call | solution.py:222
  87.4 0.0 collective-permute-done.2.down_ref
  87.4 0.0 collective-permute-done.1.over_ref
  87.4 0.0 collective-permute-done.up_ref
  87.4 0.0 collective-permute-done.6.back_ref
  87.4 0.0 collective-permute-done.5.swap_ref
  87.5 5.7 %square.1 = bf16[4,36,128,128]{3,2,1,0:T(8,128)(2,1)} custom-call(s32[16,128]{1,0:T(8,128)S(1)} %get-tuple-element.6.map_ref, bf16[4,3,128,128]{3,2,1,0:T(8,128)(2,1)S(1)} %collective-permute-done.up_ref, bf16[4,3,128,128]{3,2,1,0:T(8,128)(2,1)S(1)} %collective-permute-done.1.over_ref, bf16[4,3,128,128]{3,2,1,0:T(8,128)(2,1)S(1)} %collective-permute-done.2.down_ref, ...), custom_call_target="tpu_custom_call" | custom-call | tf_op jit(solution)/shard_map/square/pallas_call | solution.py:238
Async XLA Ops:
  0.6 22.5 %collective-permute-start.4 = (bf16[4,3,128,128]{3,2,1,0:T(8,128)(2,1)}, bf16[4,3,128,128]{3,2,1,0:T(8,128)(2,1)S(1)}, u32[]{:S(2)}, u32[]{:S(2)}) collective-permute-start(bf16[4,3,128,128]{3,2,1,0:T(8,128)(2,1)} %bitcast.13), channel_id=1, source_target_pairs={{0,504},{4,508},{8,0},{12,4},{16,8},{20,12},{24,16},{28,20},{32,24... | collective-permute-start | bytes 1179656 | tf_op jit(solution)/shard_map/ppermute | solution.py:276
  15.0 15.1 %collective-permute-start.3 = (bf16[4,3,128,128]{3,2,1,0:T(8,128)(2,1)}, bf16[4,3,128,128]{3,2,1,0:T(8,128)(2,1)S(1)}, u32[]{:S(2)}, u32[]{:S(2)}) collective-permute-start(bf16[4,3,128,128]{3,2,1,0:T(8,128)(2,1)} %bitcast.14), channel_id=1, source_target_pairs={{0,8},{4,12},{8,16},{12,20},{16,24},{20,28},{24,32},{28,36},{32,40... | collective-permute-start | bytes 1179656 | tf_op jit(solution)/shard_map/ppermute | solution.py:276
  30.2 4.9 %copy-start = (bf16[4,1,3,128,128]{4,3,2,1,0:T(8,128)(2,1)S(1)}, bf16[4,1,3,128,128]{4,3,2,1,0:T(8,128)(2,1)}, u32[]{:S(2)}) copy-start(bf16[4,1,3,128,128]{4,3,2,1,0:T(8,128)(2,1)} %param.2) | copy-start | bytes 1179652
  31.4 56.1 %collective-permute-start.5 = (bf16[3,4,3,128,128]{4,3,2,1,0:T(8,128)(2,1)S(1)}, bf16[3,4,3,128,128]{4,3,2,1,0:T(8,128)(2,1)S(1)}, u32[]{:S(2)}, u32[]{:S(2)}) collective-permute-start(bf16[3,4,3,128,128]{4,3,2,1,0:T(8,128)(2,1)S(1)} %pad_maximum_fusion.trio_ref), channel_id=1, source_target_pairs={{0,4},{4,0},{1,5},{5,1},{2,6},{6,2},{3,7},{7,3},{8,12},{12,8},{9,1... | collective-permute-start | bytes 3538952 | tf_op jit(solution)/shard_map/ppermute | solution.py:262
  35.1 17.8 %collective-permute-start.7 = (bf16[4,3,128,128]{3,2,1,0:T(8,128)(2,1)S(1)}, bf16[4,3,128,128]{3,2,1,0:T(8,128)(2,1)S(1)}, u32[]{:S(2)}, u32[]{:S(2)}) collective-permute-start(bf16[4,3,128,128]{3,2,1,0:T(8,128)(2,1)S(1)} %bitcast.16), channel_id=1, source_target_pairs={{0,500},{4,16},{8,508},{12,24},{16,4},{20,32},{24,12},{28,40},{32,... | collective-permute-start | bytes 1179656 | tf_op jit(solution)/shard_map/ppermute | solution.py:276
  37.0 50.4 %collective-permute-start.2 = (bf16[4,3,128,128]{3,2,1,0:T(8,128)(2,1)S(1)}, bf16[4,3,128,128]{3,2,1,0:T(8,128)(2,1)S(1)}, u32[]{:S(2)}, u32[]{:S(2)}) collective-permute-start(bf16[4,3,128,128]{3,2,1,0:T(8,128)(2,1)S(1)} %bitcast.17), channel_id=1, source_target_pairs={{3,0},{0,1},{1,2},{2,3},{7,4},{4,5},{5,6},{6,7},{11,8},{8,9},{9,10... | collective-permute-start | bytes 1179656 | tf_op jit(solution)/shard_map/ppermute | solution.py:266
  40.2 47.3 %collective-permute-start.1 = (bf16[4,3,128,128]{3,2,1,0:T(8,128)(2,1)S(1)}, bf16[4,3,128,128]{3,2,1,0:T(8,128)(2,1)S(1)}, u32[]{:S(2)}, u32[]{:S(2)}) collective-permute-start(bf16[4,3,128,128]{3,2,1,0:T(8,128)(2,1)S(1)} %bitcast.18), channel_id=1, source_target_pairs={{2,0},{3,1},{0,2},{1,3},{6,4},{7,5},{4,6},{5,7},{10,8},{11,9},{8,1... | collective-permute-start | bytes 1179656 | tf_op jit(solution)/shard_map/ppermute | solution.py:266
  44.5 42.9 %collective-permute-start = (bf16[4,3,128,128]{3,2,1,0:T(8,128)(2,1)S(1)}, bf16[4,3,128,128]{3,2,1,0:T(8,128)(2,1)S(1)}, u32[]{:S(2)}, u32[]{:S(2)}) collective-permute-start(bf16[4,3,128,128]{3,2,1,0:T(8,128)(2,1)S(1)} %bitcast.19), channel_id=1, source_target_pairs={{1,0},{2,1},{3,2},{0,3},{5,4},{6,5},{7,6},{4,7},{9,8},{10,9},{11,1... | collective-permute-start | bytes 1179656 | tf_op jit(solution)/shard_map/ppermute | solution.py:266
  52.9 34.5 %collective-permute-start.6 = (bf16[4,3,128,128]{3,2,1,0:T(8,128)(2,1)S(1)}, bf16[4,3,128,128]{3,2,1,0:T(8,128)(2,1)S(1)}, u32[]{:S(2)}, u32[]{:S(2)}) collective-permute-start(bf16[4,3,128,128]{3,2,1,0:T(8,128)(2,1)S(1)} %collective-permute-done.3), channel_id=1, source_target_pairs={{0,8},{4,12},{8,16},{12,20},{16,24},{20,28},{24,32},{28,36},{32,40... | collective-permute-start | bytes 1179656 | tf_op jit(solution)/shard_map/ppermute | solution.py:276
